TPU v7x, 32 devices: a whole 2x2x4 slice. The times are simulated.
32 devices in a mesh: dp: 4 (over x, core), ctx: 8 (over z, y).
Axes of the slice: x: 2, y: 2, z: 4, core: 2. Of those that a mesh axis runs over, the one named last changes fastest.
Arguments:
- tokens: bfloat16 [4096, 1792], P(('dp', 'ctx')), may hold values from -6 to 6
- cotangent: bfloat16 [4096, 1792], P(('dp', 'ctx')), may hold values from -6 to 6
- expert_ids: int32 [4096, 4], P(('dp', 'ctx')), may hold values from 0 to 15, all different within a row; in each aligned block of 128 rows (0 to 127, 128 to 255, ...) at most 40 rows name the same one
- norm_gain: float32 [1792], replicated, may hold values from 0.5 to 1.5
- router_weight: bfloat16 [1792, 16], replicated, may hold values from -0.125 to 0.125
- gate_weight: bfloat16 [16, 1792, 1536], P('ctx', None, 'dp'), may hold values from -0.125 to 0.125
- up_weight: bfloat16 [16, 1792, 1536], P('ctx', None, 'dp'), may hold values from -0.125 to 0.125
- down_weight: bfloat16 [16, 1536, 1792], P('ctx', 'dp'), may hold values from -0.15625 to 0.15625
Outputs:
- grad_tokens: bfloat16 [4096, 1792], P(('dp', 'ctx'))
- grad_gate: bfloat16 [16, 1792, 1536], P('ctx', None, 'dp')
- grad_up: bfloat16 [16, 1792, 1536], P('ctx', None, 'dp')
- grad_down: bfloat16 [16, 1536, 1792], P('ctx', 'dp')
- grad_router: float32 [1792, 16], P(('dp', 'ctx'))
- grad_gain: float32 [1792], P(('dp', 'ctx'))
Inputs may be any that keep to these rules, and one draw needn't show every extreme that they name: `expert_ids`: each row names 4 different experts; among the rows of one device no expert is named more than 40 times.
All inputs are finite; a program needn't handle non-finite values.
Results may differ from a plain program's by a relative error of at most 0.02.
Values may be sent and summed in bfloat16 or wider, within the bound.
A program may use at most 192 MiB of HBM per device.

v0:
```python
import functools

import jax
import jax.numpy as jnp
from jax import lax
from jax.experimental import pallas as pl
from jax.experimental.pallas import tpu as pltpu
from jax.sharding import PartitionSpec as P

EPSILON = 1e-05
SWISH_SCALE = 1.702
MESH = pl.DeviceIdType.MESH
ANY = pl.BlockSpec(memory_space=pl.ANY)
VMEM = pl.BlockSpec(memory_space=pltpu.VMEM)


def greet_all(n_dp, n_ctx):
    n = n_dp * n_ctx
    me = lax.axis_index("dp") * n_ctx + lax.axis_index("ctx")
    barrier = pltpu.get_barrier_semaphore()

    def hello(i, carry):
        peer = lax.rem(me + i, n)
        pl.semaphore_signal(
            barrier,
            inc=1,
            device_id=(lax.div(peer, n_ctx), lax.rem(peer, n_ctx)),
            device_id_type=MESH,
        )
        return carry

    lax.fori_loop(1, n, hello, 0)
    pl.semaphore_wait(barrier, n - 1)


def spread_copy(n_dp, n_ctx, i, src_of, land, send_sem, recv_sem, sending):
    n = n_dp * n_ctx
    me = lax.axis_index("dp") * n_ctx + lax.axis_index("ctx")
    peer = lax.rem(me + i, n)
    source = me if sending else lax.rem(me + n - i, n)
    return pltpu.make_async_remote_copy(
        src_ref=src_of(peer),
        dst_ref=land.at[source],
        send_sem=send_sem.at[i],
        recv_sem=recv_sem.at[i],
        device_id=(lax.div(peer, n_ctx), lax.rem(peer, n_ctx)),
        device_id_type=MESH,
    )


def exchange_kernel(n_dp, n_ctx, keep, x_ref, o_ref, land, send_sem, recv_sem):
    n = n_dp * n_ctx
    me = lax.axis_index("dp") * n_ctx + lax.axis_index("ctx")
    greet_all(n_dp, n_ctx)
    src_of = lambda peer: x_ref.at[peer]

    def start(i, carry):
        spread_copy(n_dp, n_ctx, i, src_of, land, send_sem, recv_sem, True).start()
        return carry

    lax.fori_loop(1, n, start, 0)
    land[pl.ds(me, 1)] = x_ref[pl.ds(me, 1)]

    def finish(i, carry):
        spread_copy(n_dp, n_ctx, i, src_of, land, send_sem, recv_sem, True).wait_send()
        spread_copy(n_dp, n_ctx, i, src_of, land, send_sem, recv_sem, False).wait_recv()
        return carry

    lax.fori_loop(1, n, finish, 0)
    o_ref[...] = jnp.sum(land[...].reshape(n // keep, keep, 8, 128), axis=0)


def exchange(x, n_dp, n_ctx, keep, cid):
    n = n_dp * n_ctx
    return pl.pallas_call(
        functools.partial(exchange_kernel, n_dp, n_ctx, keep),
        out_shape=jax.ShapeDtypeStruct((keep, 8, 128), jnp.float32),
        in_specs=[VMEM],
        out_specs=VMEM,
        scratch_shapes=[
            pltpu.VMEM((n, 8, 128), jnp.float32),
            pltpu.SemaphoreType.DMA((n,)),
            pltpu.SemaphoreType.DMA((n,)),
        ],
        compiler_params=pltpu.CompilerParams(collective_id=cid, has_side_effects=True),
    )(x)


def dispatch_kernel(
    n_dp, n_ctx, cap, rows_ref, grad_ref, gate_ref, wg_ref, wu_ref, wd_ref,
    out_rows, out_grad, out_gate, out_pre_g, out_pre_u, out_down,
    own, weights, down_held, chunk, pre, own_sem, weight_sem, chunk_sem, pre_sem,
    gate_send, gate_recv, ring_send, ring_recv, far_send, far_recv, sib_send, sib_recv,
):
    n = n_dp * n_ctx
    local = rows_ref.shape[1]
    span = n_ctx * cap
    chunks = local * n_dp
    d, c = lax.axis_index("dp"), lax.axis_index("ctx")
    me = d * n_ctx + c
    far = lax.rem(d + 2, n_dp)
    sib = d + 1 - 2 * lax.rem(d, 2)
    far_sib = lax.rem(sib + 2, n_dp)
    greet_all(n_dp, n_ctx)
    gate_src = lambda peer: gate_ref.at[lax.rem(peer, n_ctx)]
    ins, outs = (rows_ref, grad_ref), (out_rows, out_grad)

    def gate_start(i, carry):
        spread_copy(n_dp, n_ctx, i, gate_src, out_gate, gate_send, gate_recv, True).start()
        return carry

    lax.fori_loop(1, n, gate_start, 0)

    def place(a, slot):
        return outs[a].at[:, pl.ds(pl.multiple_of(slot * cap, 8), cap)]

    def ring(a, k, sending):
        peer = lax.rem(c + k, n_ctx)
        owner = c if sending else lax.rem(c + n_ctx - k, n_ctx)
        return pltpu.make_async_remote_copy(
            src_ref=ins[a].at[peer],
            dst_ref=place(a, d * n_ctx + owner),
            send_sem=ring_send.at[a, k],
            recv_sem=ring_recv.at[a, k],
            device_id=(d, peer),
            device_id_type=MESH,
        )

    def forward(a, src, slot, to, send_sem, recv_sem, index):
        return pltpu.make_async_remote_copy(
            src_ref=src,
            dst_ref=place(a, slot),
            send_sem=send_sem.at[a, index],
            recv_sem=recv_sem.at[a, index],
            device_id=(to, c),
            device_id_type=MESH,
        )

    def slot_of(row, k):
        return row * n_ctx + lax.rem(c + n_ctx - k, n_ctx)

    loads = []
    for a in range(2):
        load = pltpu.make_async_copy(ins[a].at[c], own.at[a], own_sem.at[a])
        load.start()
        loads.append(load)
    for a in range(2):

        def ring_start(k, carry, a=a):
            ring(a, k, True).start()
            return carry

        lax.fori_loop(1, n_ctx, ring_start, 0)
    wloads = [
        pltpu.make_async_copy(ref, weights.at[i], weight_sem.at[i])
        for i, ref in enumerate((wg_ref, wu_ref))
    ] + [pltpu.make_async_copy(wd_ref, down_held, weight_sem.at[2])]
    for load in wloads:
        load.start()
    stores = []
    for a in range(2):
        loads[a].wait()
        store = pltpu.make_async_copy(own.at[a], place(a, me), own_sem.at[a])
        store.start()
        stores.append(store)
    out_gate[pl.ds(me, 1)] = gate_ref[pl.ds(c, 1)]

    def near_copies(a, k, first):
        slot = slot_of(d, k)
        src = ins[a].at[c] if first else place(a, slot)
        return (
            forward(a, src, slot, far, far_send, far_recv, k),
            forward(a, src, slot, sib, sib_send, sib_recv, k),
        )

    def sib_copy(a, k):
        slot = slot_of(far, k)
        return forward(a, place(a, slot), slot, sib, sib_send, sib_recv, n_ctx + k)

    def await_far(a, k):
        slot = slot_of(far, k)
        forward(a, place(a, slot), slot, far, far_send, far_recv, k).wait_recv()

    def await_sib(a):
        def wait(k, carry):
            slot = slot_of(sib, k)
            forward(a, place(a, slot), slot, sib, sib_send, sib_recv, k).wait_recv()
            slot = slot_of(far_sib, k)
            forward(a, place(a, slot), slot, sib, sib_send, sib_recv, n_ctx + k).wait_recv()
            return carry

        lax.fori_loop(0, n_ctx, wait, 0)

    def step(a, k):
        @pl.when(k < n_ctx)
        def _():
            ring(a, k, False).wait_recv()
            for copy in near_copies(a, k, False):
                copy.start()

        await_far(a, k - 1)
        sib_copy(a, k - 1).start()

    def chunk_at(u):
        q = lax.div(u, local)
        row = lax.rem(d + lax.div(q, 2) * (sib - d) + 2 * lax.rem(q, 2), n_dp)
        return lax.rem(u, local), pl.ds(pl.multiple_of(row * span, 8), span)

    def chunk_load(a, u):
        return pltpu.make_async_copy(
            outs[a].at[chunk_at(u)],
            chunk.at[lax.rem(u, 2)],
            chunk_sem.at[lax.rem(u, 2)],
        )

    def chunk_out(u, i):
        return pltpu.make_async_copy(
            pre.at[i, u],
            (out_pre_g, out_pre_u, out_down)[i].at[chunk_at(u)],
            pre_sem.at[i, u],
        )

    def compute(u, carry):
        chunk_load(0, u).wait()

        @pl.when(u + 1 < chunks)
        def _():
            chunk_load(0, u + 1).start()

        held = chunk[lax.rem(u, 2)]
        for i in range(2):
            pre[i, u] = jnp.dot(
                held, weights[i, lax.rem(u, local)], preferred_element_type=jnp.float32
            )
            chunk_out(u, i).start()
        return carry

    def compute_down(u, carry):
        chunk_load(1, u).wait()

        @pl.when(u + 1 < chunks)
        def _():
            chunk_load(1, u + 1).start()

        pre[2, u] = lax.dot_general(
            chunk[lax.rem(u, 2)],
            down_held[lax.rem(u, local)],
            (((1,), (1,)), ((), ())),
            preferred_element_type=jnp.float32,
        )
        chunk_out(u, 2).start()
        return carry

    def first(k, carry):
        step(0, k)
        return carry

    for copy in near_copies(0, 0, True):
        copy.start()
    lax.fori_loop(1, n_ctx + 1, first, 0)
    for copy in near_copies(1, 0, True):
        copy.start()
    stores[0].wait()
    await_sib(0)
    for load in wloads:
        load.wait()
    chunk_load(0, 0).start()

    def second(k, carry):
        step(1, k)
        lax.fori_loop(lax.div((k - 1) * chunks, n_ctx), lax.div(k * chunks, n_ctx), compute, 0)
        return carry

    lax.fori_loop(1, n_ctx + 1, second, 0)
    await_sib(1)
    stores[1].wait()
    chunk_load(1, 0).start()
    lax.fori_loop(0, chunks, compute_down, 0)
    for a in range(2):
        for copy in near_copies(a, 0, True):
            copy.wait_send()
        sib_copy(a, 0).wait_send()

        def drain(k, carry, a=a):
            ring(a, k, True).wait_send()
            for copy in near_copies(a, k, False):
                copy.wait_send()
            sib_copy(a, k).wait_send()
            return carry

        lax.fori_loop(1, n_ctx, drain, 0)

    def pre_finish(u, carry):
        for i in range(3):
            chunk_out(u, i).wait()
        return carry

    lax.fori_loop(0, chunks, pre_finish, 0)

    def gate_finish(i, carry):
        spread_copy(n_dp, n_ctx, i, gate_src, out_gate, gate_send, gate_recv, True).wait_send()
        spread_copy(n_dp, n_ctx, i, gate_src, out_gate, gate_send, gate_recv, False).wait_recv()
        return carry

    lax.fori_loop(1, n, gate_finish, 0)


def dispatch_rows(rows, grad, gate, gate_weight, up_weight, down_weight, n_dp, n_ctx):
    n = n_dp * n_ctx
    _, local, cap, width = rows.shape
    hidden = gate_weight.shape[2]
    arrived = jax.ShapeDtypeStruct((local, n * cap, width), rows.dtype)
    pre = jax.ShapeDtypeStruct((local, n * cap, hidden), jnp.float32)
    return pl.pallas_call(
        functools.partial(dispatch_kernel, n_dp, n_ctx, cap),
        out_shape=(arrived, arrived, jax.ShapeDtypeStruct((n, 8, 128), jnp.float32))
        + (pre,) * 3,
        in_specs=[ANY, ANY, VMEM, ANY, ANY, ANY],
        out_specs=(ANY, ANY, VMEM, ANY, ANY, ANY),
        scratch_shapes=[
            pltpu.VMEM((2, local, cap, width), rows.dtype),
            pltpu.VMEM((2,) + gate_weight.shape, gate_weight.dtype),
            pltpu.VMEM(down_weight.shape, down_weight.dtype),
            pltpu.VMEM((2, n_ctx * cap, width), rows.dtype),
            pltpu.VMEM((3, local * n_dp, n_ctx * cap, hidden), jnp.float32),
            pltpu.SemaphoreType.DMA((2,)),
            pltpu.SemaphoreType.DMA((3,)),
            pltpu.SemaphoreType.DMA((2,)),
            pltpu.SemaphoreType.DMA((3, local * n_dp)),
            pltpu.SemaphoreType.DMA((n,)),
            pltpu.SemaphoreType.DMA((n,)),
            pltpu.SemaphoreType.DMA((2, n_ctx)),
            pltpu.SemaphoreType.DMA((2, n_ctx)),
            pltpu.SemaphoreType.DMA((2, n_ctx)),
            pltpu.SemaphoreType.DMA((2, n_ctx)),
            pltpu.SemaphoreType.DMA((2, 2 * n_ctx)),
            pltpu.SemaphoreType.DMA((2, 2 * n_ctx)),
        ],
        compiler_params=pltpu.CompilerParams(
            collective_id=0, has_side_effects=True, vmem_limit_bytes=48 * 1024 * 1024
        ),
    )(rows, grad, gate, gate_weight, up_weight, down_weight)


def return_kernel(
    n_dp, n_ctx, cap, tile, back_ref, rows_ref, grad_ref, pg_ref, pu_ref, hid_ref, score_ref,
    out_ref, gate_out, up_out, down_out, out_score,
    mine, sib_land, far_out, far_land, done, pair, hid_raw, hid, row_tile, grad_tile, both, down,
    mine_sem, sib_send, sib_recv, far_send, far_recv, ring_send, ring_recv, own_sem,
    hold_sem, tile_sem, result_sem, score_send, score_recv,
):
    d, c = lax.axis_index("dp"), lax.axis_index("ctx")
    local = back_ref.shape[0]
    width, depth = rows_ref.shape[2], pg_ref.shape[2]
    across = width // tile
    units = local * across
    far = lax.rem(d + 2, n_dp)
    sib = d + 1 - 2 * lax.rem(d, 2)
    far_sib = lax.rem(sib + 2, n_dp)
    greet_all(n_dp, n_ctx)

    def dest(k):
        return lax.rem(c + k, n_ctx)

    def block(slot):
        return back_ref.at[:, pl.ds(pl.multiple_of(slot * cap, 8), cap)]

    def to_sib(k, which):
        row = far_sib if which == 0 else sib
        return pltpu.make_async_remote_copy(
            src_ref=block(row * n_ctx + dest(k)),
            dst_ref=sib_land.at[k, which],
            send_sem=sib_send.at[k, which],
            recv_sem=sib_recv.at[k, which],
            device_id=(sib, c),
            device_id_type=MESH,
        )

    def load(k, which):
        row = far if which == 0 else d
        return pltpu.make_async_copy(
            block(row * n_ctx + dest(k)), mine.at[k, which], mine_sem.at[k, which]
        )

    def to_far(k):
        return pltpu.make_async_remote_copy(
            src_ref=far_out.at[k],
            dst_ref=far_land.at[k],
            send_sem=far_send.at[k],
            recv_sem=far_recv.at[k],
            device_id=(far, c),
            device_id_type=MESH,
        )

    def ring(k, sending):
        owner = c if sending else lax.rem(c + n_ctx - k, n_ctx)
        return pltpu.make_async_remote_copy(
            src_ref=done.at[k],
            dst_ref=out_ref.at[owner],
            send_sem=ring_send.at[k],
            recv_sem=ring_recv.at[k],
            device_id=(d, dest(k)),
            device_id_type=MESH,
        )

    gaps = n_ctx + 1

    def turn(i):
        return lax.rem(i + 1, n_ctx)

    def tile_loads(u):
        e, slot = lax.div(u, across), lax.rem(u, 2)
        columns = pl.ds(pl.multiple_of(lax.rem(u, across) * tile, tile), tile)
        return (
            pltpu.make_async_copy(
                rows_ref.at[e, :, columns], row_tile.at[slot], tile_sem.at[0, slot]
            ),
            pltpu.make_async_copy(
                grad_ref.at[e, :, columns], grad_tile.at[slot], tile_sem.at[1, slot]
            ),
        )

    def results(u):
        e = lax.div(u, across)
        columns = pl.ds(pl.multiple_of(lax.rem(u, across) * tile, tile), tile)
        return (
            pltpu.make_async_copy(
                both.at[u, :, pl.ds(0, depth)], gate_out.at[e, columns], result_sem.at[0, u]
            ),
            pltpu.make_async_copy(
                both.at[u, :, pl.ds(depth, depth)], up_out.at[e, columns], result_sem.at[1, u]
            ),
            pltpu.make_async_copy(down.at[u], down_out.at[e, :, columns], result_sem.at[2, u]),
        )

    def unit(u, carry):
        for copy in tile_loads(u):
            copy.wait()

        @pl.when(u + 1 < units)
        def _():
            for copy in tile_loads(u + 1):
                copy.start()

        e, slot = lax.div(u, across), lax.rem(u, 2)
        both[u] = jnp.dot(
            row_tile[slot].T, pair[e], preferred_element_type=jnp.float32
        ).astype(jnp.bfloat16)
        down[u] = jnp.dot(
            hid[e], grad_tile[slot], preferred_element_type=jnp.float32
        ).astype(jnp.bfloat16)
        for copy in results(u):
            copy.start()
        return carry

    n = n_dp * n_ctx
    me = d * n_ctx + c
    score_src = lambda peer: score_ref.at[peer]

    def score_start(i, carry):
        spread_copy(n_dp, n_ctx, i, score_src, out_score, score_send, score_recv, True).start()
        return carry

    def score_finish(i, carry):
        spread_copy(n_dp, n_ctx, i, score_src, out_score, score_send, score_recv, True).wait_send()
        spread_copy(n_dp, n_ctx, i, score_src, out_score, score_send, score_recv, False).wait_recv()
        return carry

    def begin(i, carry):
        k = turn(i)
        for which in range(2):
            to_sib(k, which).start()
            load(k, which).start()
        return carry

    lax.fori_loop(0, n_ctx, begin, 0)
    holds = (
        pltpu.make_async_copy(pg_ref, pair.at[:, :, pl.ds(0, depth)], hold_sem.at[0]),
        pltpu.make_async_copy(pu_ref, pair.at[:, :, pl.ds(depth, depth)], hold_sem.at[1]),
        pltpu.make_async_copy(hid_ref, hid_raw, hold_sem.at[2]),
    )
    for copy in holds:
        copy.start()
    for copy in tile_loads(0):
        copy.start()

    def outward(i, carry):
        k = turn(i)
        to_sib(k, 0).wait_recv()
        load(k, 0).wait()
        far_out[k] = (
            mine[k, 0].astype(jnp.float32) + sib_land[k, 0].astype(jnp.float32)
        ).astype(jnp.bfloat16)
        to_far(k).start()
        return carry

    lax.fori_loop(0, n_ctx, outward, 0)
    lax.fori_loop(1, n, score_start, 0)
    out_score[pl.ds(me, 1)] = score_ref[pl.ds(me, 1)]
    for copy in holds:
        copy.wait()
    for e in range(local):
        hid[e] = hid_raw[e].T

    def inward(i, carry):
        k = turn(i)
        lax.fori_loop(lax.div(i * units, gaps), lax.div((i + 1) * units, gaps), unit, 0)
        to_sib(k, 1).wait_recv()
        load(k, 1).wait()
        to_far(k).wait_recv()
        done[k] = (
            mine[k, 1].astype(jnp.float32)
            + sib_land[k, 1].astype(jnp.float32)
            + far_land[k].astype(jnp.float32)
        ).astype(jnp.bfloat16)

        @pl.when(k > 0)
        def _():
            ring(k, True).start()

        return carry

    lax.fori_loop(0, n_ctx, inward, 0)
    own = pltpu.make_async_copy(done.at[0], out_ref.at[c], own_sem)
    own.start()
    lax.fori_loop(n_ctx * units // gaps, units, unit, 0)
    own.wait()
    lax.fori_loop(1, n, score_finish, 0)

    def drain(k, carry):
        to_sib(k, 0).wait_send()
        to_sib(k, 1).wait_send()
        to_far(k).wait_send()

        @pl.when(k > 0)
        def _():
            ring(k, True).wait_send()
            ring(k, False).wait_recv()

        return carry

    lax.fori_loop(0, n_ctx, drain, 0)

    def store_wait(u, carry):
        for copy in results(u):
            copy.wait()
        return carry

    lax.fori_loop(0, units, store_wait, 0)


def return_rows(back, rows, grad, pre_gate, pre_up, hidden, score, n_dp, n_ctx):
    local, total, width = back.shape
    cap = total // (n_dp * n_ctx)
    depth = pre_gate.shape[2]
    tile = 256 if width % 256 == 0 else 128
    units = local * (width // tile)
    block = (local, cap, width)
    low = back.dtype
    return pl.pallas_call(
        functools.partial(return_kernel, n_dp, n_ctx, cap, tile),
        out_shape=(
            jax.ShapeDtypeStruct((n_ctx,) + block, low),
            jax.ShapeDtypeStruct((local, width, depth), low),
            jax.ShapeDtypeStruct((local, width, depth), low),
            jax.ShapeDtypeStruct((local, depth, width), low),
            jax.ShapeDtypeStruct((n_dp * n_ctx, 8, 128), jnp.float32),
        ),
        in_specs=[ANY] * 6 + [VMEM],
        out_specs=(ANY,) * 4 + (VMEM,),
        scratch_shapes=[
            pltpu.VMEM((n_ctx, 2) + block, low),
            pltpu.VMEM((n_ctx, 2) + block, low),
            pltpu.VMEM((n_ctx,) + block, low),
            pltpu.VMEM((n_ctx,) + block, low),
            pltpu.VMEM((n_ctx,) + block, low),
            pltpu.VMEM((local, total, 2 * depth), low),
            pltpu.VMEM((local, total, depth), low),
            pltpu.VMEM((local, depth, total), low),
            pltpu.VMEM((2, total, tile), low),
            pltpu.VMEM((2, total, tile), low),
            pltpu.VMEM((units, tile, 2 * depth), low),
            pltpu.VMEM((units, depth, tile), low),
            pltpu.SemaphoreType.DMA((n_ctx, 2)),
            pltpu.SemaphoreType.DMA((n_ctx, 2)),
            pltpu.SemaphoreType.DMA((n_ctx, 2)),
            pltpu.SemaphoreType.DMA((n_ctx,)),
            pltpu.SemaphoreType.DMA((n_ctx,)),
            pltpu.SemaphoreType.DMA((n_ctx,)),
            pltpu.SemaphoreType.DMA((n_ctx,)),
            pltpu.SemaphoreType.DMA,
            pltpu.SemaphoreType.DMA((3,)),
            pltpu.SemaphoreType.DMA((2, 2)),
            pltpu.SemaphoreType.DMA((3, units)),
            pltpu.SemaphoreType.DMA((n_dp * n_ctx,)),
            pltpu.SemaphoreType.DMA((n_dp * n_ctx,)),
        ],
        compiler_params=pltpu.CompilerParams(
            collective_id=1, has_side_effects=True, vmem_limit_bytes=60 * 1024 * 1024
        ),
    )(back, rows, grad, pre_gate, pre_up, hidden, score)


def expert_pass(gate_pre, up_pre, grad_out, weight, gate_weight, up_weight):
    squash = jax.nn.sigmoid(SWISH_SCALE * gate_pre)
    full = gate_pre * squash * (up_pre + 1.0)
    hidden = full.astype(jnp.bfloat16)
    hidden_scaled = (weight[:, :, None] * full).astype(jnp.bfloat16)
    score = jnp.sum(grad_out * hidden.astype(jnp.float32), axis=2)
    grad_hidden = weight[:, :, None] * grad_out
    slope = squash + SWISH_SCALE * gate_pre * squash * (1.0 - squash)
    grad_pre_gate = (grad_hidden * (up_pre + 1.0) * slope).astype(jnp.bfloat16)
    grad_pre_up = (grad_hidden * gate_pre * squash).astype(jnp.bfloat16)
    back = jnp.einsum(
        "prf,pdf->prd", grad_pre_gate, gate_weight, preferred_element_type=jnp.float32
    )
    back = back + jnp.einsum(
        "prf,pdf->prd", grad_pre_up, up_weight, preferred_element_type=jnp.float32
    )
    return (grad_pre_gate, grad_pre_up, hidden_scaled, back.astype(jnp.bfloat16), score)


def tiles(x):
    return jnp.pad(x, ((0, 0), (0, 1024 - x.shape[1]))).reshape(x.shape[0], 8, 128)


def body(
    tokens, cotangent, expert_ids, norm_gain, router_weight, gate_weight, up_weight, down_weight
):
    n_ctx = lax.axis_size("ctx")
    n_dp = lax.axis_size("dp")
    n = n_dp * n_ctx
    local = gate_weight.shape[0]
    experts = router_weight.shape[1]
    rows_here = tokens.shape[0]
    picks = expert_ids.shape[1]
    width = tokens.shape[1]
    assigned = rows_here * picks
    capacity = max(2, rows_here * picks * 5 // (4 * experts))
    capacity = -(-capacity // 8) * 8
    slots = experts * capacity
    widened = tokens.astype(jnp.float32)
    inverse = lax.rsqrt(jnp.mean(widened * widened, axis=1, keepdims=True) + EPSILON)
    scaled = widened * inverse
    normed = (scaled * norm_gain).astype(jnp.bfloat16)
    logits = jnp.dot(normed, router_weight, preferred_element_type=jnp.float32)
    labels = jnp.arange(experts, dtype=jnp.int32)
    member = expert_ids[:, :, None] == labels
    chosen = jnp.sum(jnp.where(member, logits[:, None, :], 0.0), axis=2)
    lifted = jnp.exp(chosen)
    gates = lifted / jnp.sum(lifted, axis=1, keepdims=True)
    hits = member.reshape(assigned, experts).astype(jnp.int32)
    rank = jnp.sum((jnp.cumsum(hits, axis=0) - 1) * hits, axis=1)
    position = expert_ids.reshape(-1) * capacity + rank
    match = (jnp.arange(slots, dtype=jnp.int32)[:, None] == position[None, :]).astype(jnp.float32)
    dispatch = jnp.sum(match.reshape(slots, rows_here, picks), axis=2)
    dispatch_low = dispatch.astype(jnp.bfloat16)
    out_rows = jnp.dot(dispatch_low, normed, preferred_element_type=jnp.float32).astype(
        jnp.bfloat16
    )
    out_rows = out_rows.reshape(n_ctx, local, capacity, width)
    out_grad = jnp.dot(dispatch_low, cotangent, preferred_element_type=jnp.float32).astype(
        jnp.bfloat16
    )
    out_grad = out_grad.reshape(n_ctx, local, capacity, width)
    out_gate = jnp.dot(match, gates.reshape(-1), precision=lax.Precision.HIGHEST)
    out_gate = tiles(out_gate.reshape(n_ctx, local * capacity))
    rows, upstream, weight, gate_pre, up_pre, grad_out = dispatch_rows(
        out_rows, out_grad, out_gate, gate_weight, up_weight, down_weight, n_dp, n_ctx
    )
    weight = weight.reshape(n, 1024)[:, : local * capacity].reshape(n, local, capacity)
    weight = weight.transpose(1, 0, 2).reshape(local, n * capacity)
    pre_gate, pre_up, hidden, back, score = expert_pass(
        gate_pre, up_pre, grad_out, weight, gate_weight, up_weight
    )
    score_out = score.reshape(local, n, capacity).transpose(1, 0, 2).reshape(n, local * capacity)
    back_slots, gate_grad, up_grad, down_grad, score_parts = return_rows(
        back, rows, upstream, pre_gate, pre_up, hidden, tiles(score_out), n_dp, n_ctx
    )
    score_slots = jnp.sum(score_parts.reshape(n_dp, n_ctx, 8, 128), axis=0)
    back_flat = back_slots.reshape(slots, width)
    score_flat = score_slots.reshape(n_ctx, 1024)[:, : local * capacity].reshape(slots)
    grad_tok = jnp.dot(dispatch_low.T, back_flat, preferred_element_type=jnp.float32)
    score_tok = jnp.dot(score_flat, match, precision=lax.Precision.HIGHEST).reshape(
        rows_here, picks
    )
    mixed = jnp.sum(gates * score_tok, axis=1, keepdims=True)
    grad_chosen = gates * (score_tok - mixed)
    grad_logits = jnp.sum(jnp.where(member, grad_chosen[:, :, None], 0.0), axis=1).astype(
        jnp.bfloat16
    )
    grad_normed = grad_tok + jnp.dot(
        grad_logits, router_weight.T, preferred_element_type=jnp.float32
    )
    router_part = jnp.dot(normed.T, grad_logits, preferred_element_type=jnp.float32)
    gain_part = jnp.sum(grad_normed * scaled, axis=0)
    share = width // n
    parts = jnp.concatenate(
        [router_part.reshape(n, share * experts), gain_part.reshape(n, share)], axis=1
    )
    sums = exchange(tiles(parts), n_dp, n_ctx, 1, 3).reshape(1024)
    router_grad = sums[: share * experts].reshape(share, experts)
    gain_grad = sums[share * experts : share * experts + share]
    grad_scaled = grad_normed * norm_gain
    correction = jnp.mean(grad_scaled * scaled, axis=1, keepdims=True)
    grad_input = (
        cotangent.astype(jnp.float32) + inverse * (grad_scaled - scaled * correction)
    ).astype(jnp.bfloat16)
    return (grad_input, gate_grad, up_grad, down_grad, router_grad, gain_grad)


def solution(mesh):
    return jax.shard_map(
        body,
        mesh=mesh,
        in_specs=(
            P(("dp", "ctx"), None),
            P(("dp", "ctx"), None),
            P(("dp", "ctx"), None),
            P(),
            P(),
            P("ctx", None, "dp"),
            P("ctx", None, "dp"),
            P("ctx", "dp", None),
        ),
        out_specs=(
            P(("dp", "ctx"), None),
            P("ctx", None, "dp"),
            P("ctx", None, "dp"),
            P("ctx", "dp", None),
            P(("dp", "ctx"), None),
            P(("dp", "ctx")),
        ),
        check_vma=False,
    )
```

profile of v0, /device:TPU:0, one launch (start us, length us, event | category | flops | bytes accessed | tf_op | source)
XLA Modules:
  0.0 308.4 jit_solution(15478685381619324492)
XLA Ops:
  0.7 1.3 fusion.13
  2.0 1.3 fusion.28
  3.2 0.8 select_reduce_fusion.2
  4.3 0.8 copy.51
  5.2 1.2 reduce-window.6
  6.8 0.8 fusion
  7.9 0.7 multiply_add_fusion.2
  8.7 1.5 convolution_convert_fusion.1
  10.3 0.7 convolution_convert_fusion
  11.0 141.2 %shard_map.127 = (bf16[2,1280,1792]{2,1,0:T(8,128)(2,1)}, bf16[2,1280,1792]{2,1,0:T(8,128)(2,1)}, f32[32,8,128]{2,1,0:T(8,128)S(1)}, f32[2,1280,384]{2,1,0:T(8,1...) custom-call(bf16[8,2,40,1792]{3,2,1,0:T(8,128)(2,1)S(1)} %bitcast.62, bf16[8,2,40,1792]{3,2,1,0:T(8,128)(2,1)S(1)} %bitcast.63, ...), custom_call_target="tpu_custom_call" | custom-call | tf_op jit(solution)/shard_map/pallas_call | solution.py:314
  152.5 7.2 %multiply_reduce_fusion = (f32[2,1280]{1,0:T(2,128)S(1)}, bf16[2,1280,384]{2,1,0:T(8,128)(2,1)S(1)}, bf16[2,1280,384]{2,1,0:T(8,128)(2,1)}, bf16[2,1280,384]{2,1,0:T(8,128)(2,1)S(1)}) fusion(f32[2,1280,384]{2,1,0:T(8,128)} %get-tuple-element.18, f32[2,1280,384]{2,1,0:T(8,128)} %get-tuple-element.19, f32[2,1280,384]{2,1,0:T(8,128)} %get-tuple-element.20, ...), kind=kLoop, calls=%fused_computation.1 | loop fusion | flops 23590400 | bytes 17715200 | tf_op jit(solution)/shard_map/reduce_sum | solution.py:609
  159.8 8.9 %fusion.31 = f32[2,1280,1792]{2,1,0:T(8,128)} fusion(bf16[2,1280,384]{2,1,0:T(8,128)(2,1)S(1)} %get-tuple-element.61.pg_ref, bf16[2,1792,384]{2,1,0:T(8,128)(2,1)S(1)} %copy-done.4), kind=kOutput, calls=%fused_computation.69 | convolution fusion | flops 3523215360 | bytes 23068672 | tf_op jit(solution)/shard_map/prf,pdf->prd/dot_general | solution.py:614
  168.7 11.8 %add_convert_fusion.back_ref = bf16[2,1280,1792]{2,1,0:T(8,128)(2,1)} fusion(f32[2,1280,1792]{2,1,0:T(8,128)} %fusion.31, bf16[2,1280,384]{2,1,0:T(8,128)(2,1)S(1)} %get-tuple-element.63.pu_ref, bf16[2,1792,384]{2,1,0:T(8,128)(2,1)} %wu_ref.1), kind=kOutput, calls=%fused_computation | convolution fusion | flops 3532390400 | bytes 32243712 | tf_op jit(solution)/shard_map/prf,pdf->prd/dot_general | solution.py:617
  181.4 92.9 %shard_map.128 = (bf16[8,2,40,1792]{3,2,1,0:T(8,128)(2,1)}, bf16[2,1792,384]{2,1,0:T(8,128)(2,1)}, bf16[2,1792,384]{2,1,0:T(8,128)(2,1)}, bf16[2,384,1792]{2,1,0:T(8,128)(2,1)}, f32[32,8,128]{2,1,0:T(8,128)}) custom-call(bf16[2,1280,1792]{2,1,0:T(8,128)(2,1)} %add_convert_fusion.back_ref, bf16[2,1280,1792]{2,1,0:T(8,128)(2,1)} %get-tuple-element.21.rows_ref, ...), custom_call_target="tpu_custom_call" | custom-call | tf_op jit(solution)/shard_map/pallas_call | solution.py:560
  274.3 0.9 reduce_sum.108
  277.1 2.2 fusion.32
  280.6 16.0 %shard_map.129 = f32[1,8,128]{2,1,0:T(8,128)} custom-call(f32[32,8,128]{2,1,0:T(8,128)} %bitcast.68), custom_call_target="tpu_custom_call" | custom-call | tf_op jit(solution)/shard_map/pallas_call | solution.py:75
  296.6 0.7 reshape.191
  298.1 1.2 slice.24
  299.3 1.1 fusion.11
  300.4 3.7 %copy.85 = bf16[2,1792,384]{2,1,0:T(8,128)(2,1)} copy(bf16[2,1792,384]{2,1,0:T(8,128)(2,1)} %get-tuple-element.72) | data formatting | bytes 5505024
  304.1 1.5 copy.86
  305.7 1.2 copy-done.5
  306.9 1.5 copy.87
  (66 shorter events, 6.1 us)
Async XLA Ops:
  0.6 1.3 copy-start
  0.6 8.1 %copy-start.3 = (bf16[128,1792]{1,0:T(8,128)(2,1)S(1)}, bf16[128,1792]{1,0:T(8,128)(2,1)}, u32[]{:S(2)}) copy-start(bf16[128,1792]{1,0:T(8,128)(2,1)} %param.8) | copy-start | bytes 1376260
  0.7 9.6 %copy-start.7 = (bf16[128,1792]{1,0:T(8,128)(2,1)S(1)}, bf16[128,1792]{1,0:T(8,128)(2,1)}, u32[]{:S(2)}) copy-start(bf16[128,1792]{1,0:T(8,128)(2,1)} %param.9) | copy-start | bytes 1376260
  152.5 7.3 %copy-start.4 = (bf16[2,1792,384]{2,1,0:T(8,128)(2,1)S(1)}, bf16[2,1792,384]{2,1,0:T(8,128)(2,1)}, u32[]{:S(2)}) copy-start(bf16[2,1792,384]{2,1,0:T(8,128)(2,1)} %wg_ref.1) | copy-start | bytes 8257540
  159.8 8.9 %copy-start.2 = (bf16[2,1280,384]{2,1,0:T(8,128)(2,1)}, bf16[2,1280,384]{2,1,0:T(8,128)(2,1)S(1)}, u32[]{:S(2)}) copy-start(bf16[2,1280,384]{2,1,0:T(8,128)(2,1)S(1)} %get-tuple-element.61.pg_ref) | copy-start | bytes 5898244
  159.8 8.9 %copy-start.1 = (bf16[2,1280,384]{2,1,0:T(8,128)(2,1)}, bf16[2,1280,384]{2,1,0:T(8,128)(2,1)S(1)}, u32[]{:S(2)}) copy-start(bf16[2,1280,384]{2,1,0:T(8,128)(2,1)S(1)} %get-tuple-element.63.pu_ref) | copy-start | bytes 5898244
  181.4 95.0 %copy-start.9 = (s32[128,4]{0,1:T(4,128)S(1)}, s32[128,4]{0,1:T(4,128)}, u32[]{:S(2)}) copy-start(s32[128,4]{0,1:T(4,128)} %param.10) | copy-start | bytes 6148
  181.4 95.0 %copy-start.8 = (f32[1792]{0:T(1024)S(1)}, f32[1792]{0:T(1024)}, u32[]{:S(2)}) copy-start(f32[1792]{0:T(1024)} %param.11) | copy-start | bytes 21508
  300.4 3.7 %copy-start.6 = (bf16[2,1792,384]{2,1,0:T(8,128)(2,1)S(1)}, bf16[2,1792,384]{2,1,0:T(8,128)(2,1)}, u32[]{:S(2)}) copy-start(bf16[2,1792,384]{2,1,0:T(8,128)(2,1)} %get-tuple-element.73) | copy-start | bytes 8257540
  304.1 2.8 copy-start.5
where the time goes:
time: 309 us; the launch traced here: 308 us
  Pallas kernels  250 us (81%)
  matrix products  28.2 us (9%)
  local copies, waits for them, and re-layouts  14.8 us (5%)
  other arithmetic  14.3 us (5%)
    pallas_call x1, Pallas kernels, dispatch_rows(): pl.pallas_call(functools.partial(dispatch_kernel, n_dp, n_ctx, cap), out_...  141 us
    pallas_call x1, Pallas kernels, return_rows(): pl.pallas_call(functools.partial(return_kernel, n_dp, n_ctx, cap, tile),...  92.9 us
    pallas_call x1, Pallas kernels, exchange(): pl.pallas_call(functools.partial(exchange_kernel, n_dp, n_ctx, keep), out...  16 us
    dot_general x1, matrix products, expert_pass(): jnp.einsum('prf,pdf->prd', grad_pre_up, up_weight, preferred_element_type...  11.8 us
    unnamed x32, local copies, waits for them, and re-layouts  11 us
    dot_general x1, matrix products, expert_pass(): jnp.einsum('prf,pdf->prd', grad_pre_gate, gate_weight, preferred_element_...  8.88 us
    reduce_sum x1, other arithmetic, expert_pass(): score = jnp.sum(grad_out * hidden.astype(jnp.float32), axis=2)  7.24 us

commit v1 on v0

v1 whole, which is shorter than its diff:
```python
import functools

import jax
import jax.numpy as jnp
from jax import lax
from jax.experimental import pallas as pl
from jax.experimental.pallas import tpu as pltpu
from jax.sharding import PartitionSpec as P

EPSILON = 1e-05
SWISH_SCALE = 1.702
INNER = 2
MESH = pl.DeviceIdType.MESH
ANY = pl.BlockSpec(memory_space=pl.ANY)
VMEM = pl.BlockSpec(memory_space=pltpu.VMEM)


def greet_all(n_dp, n_ctx):
    n = n_dp * n_ctx
    me = lax.axis_index("dp") * n_ctx + lax.axis_index("ctx")
    barrier = pltpu.get_barrier_semaphore()

    def hello(i, carry):
        peer = lax.rem(me + i, n)
        pl.semaphore_signal(
            barrier,
            inc=1,
            device_id=(lax.div(peer, n_ctx), lax.rem(peer, n_ctx)),
            device_id_type=MESH,
        )
        return carry

    lax.fori_loop(1, n, hello, 0)
    pl.semaphore_wait(barrier, n - 1)


def spread_copy(n_dp, n_ctx, i, src_of, land, send_sem, recv_sem, sending):
    n = n_dp * n_ctx
    me = lax.axis_index("dp") * n_ctx + lax.axis_index("ctx")
    peer = lax.rem(me + i, n)
    source = me if sending else lax.rem(me + n - i, n)
    return pltpu.make_async_remote_copy(
        src_ref=src_of(peer),
        dst_ref=land.at[source],
        send_sem=send_sem.at[i],
        recv_sem=recv_sem.at[i],
        device_id=(lax.div(peer, n_ctx), lax.rem(peer, n_ctx)),
        device_id_type=MESH,
    )


def exchange_kernel(n_dp, n_ctx, keep, x_ref, o_ref, land, send_sem, recv_sem):
    n = n_dp * n_ctx
    me = lax.axis_index("dp") * n_ctx + lax.axis_index("ctx")
    greet_all(n_dp, n_ctx)
    src_of = lambda peer: x_ref.at[peer]

    def start(i, carry):
        spread_copy(n_dp, n_ctx, i, src_of, land, send_sem, recv_sem, True).start()
        return carry

    lax.fori_loop(1, n, start, 0)
    land[pl.ds(me, 1)] = x_ref[pl.ds(me, 1)]

    def finish(i, carry):
        spread_copy(n_dp, n_ctx, i, src_of, land, send_sem, recv_sem, True).wait_send()
        spread_copy(n_dp, n_ctx, i, src_of, land, send_sem, recv_sem, False).wait_recv()
        return carry

    lax.fori_loop(1, n, finish, 0)
    o_ref[...] = jnp.sum(land[...].reshape(n // keep, keep, 8, 128), axis=0)


def exchange(x, n_dp, n_ctx, keep, cid):
    n = n_dp * n_ctx
    return pl.pallas_call(
        functools.partial(exchange_kernel, n_dp, n_ctx, keep),
        out_shape=jax.ShapeDtypeStruct((keep, 8, 128), jnp.float32),
        in_specs=[VMEM],
        out_specs=VMEM,
        scratch_shapes=[
            pltpu.VMEM((n, 8, 128), jnp.float32),
            pltpu.SemaphoreType.DMA((n,)),
            pltpu.SemaphoreType.DMA((n,)),
        ],
        compiler_params=pltpu.CompilerParams(collective_id=cid, has_side_effects=True),
    )(x)


def line_of(c, n_ctx):
    return lax.div(c, INNER), lax.rem(c, INNER), n_ctx // INNER


def line_step(z, length, q):
    near = jnp.minimum(z, length - 1 - z)
    around = z + lax.div(q + 1, 2) * (1 - 2 * lax.rem(q, 2))
    beyond = jnp.where(z < length - 1 - z, q, length - 1 - q)
    return jnp.where(q <= 2 * near, around, beyond)


def slot_masks(meta, picks, cap, base):
    places = (lax.broadcasted_iota(jnp.int32, (cap, meta.shape[1]), 0) + base).astype(jnp.float32)
    return [meta[k : k + 1] == places for k in range(picks)]


def dispatch_kernel(
    n_dp, n_ctx, cap, rows_ref, grad_ref, meta_ref, wg_ref, wu_ref, wd_ref,
    out_rows, out_grad, out_pair, out_hid, out_back, out_score,
    dense, meta_all, sel_own, sel_side, pair_w, down_w, chunk, pair_out, hid_out, back_out,
    meta_send, meta_recv, own_sem, weight_sem, line_send, line_recv, side_send, side_recv,
    far_send, far_recv, sib_send, sib_recv, store_sem, chunk_sem, result_sem,
):
    n = n_dp * n_ctx
    local, depth = wd_ref.shape[0], wd_ref.shape[1]
    picks = meta_ref.shape[1] // 2
    d, c = lax.axis_index("dp"), lax.axis_index("ctx")
    z, y, length = line_of(c, n_ctx)
    me = d * n_ctx + c
    side = z * INNER + 1 - y
    far = lax.rem(d + 2, n_dp)
    sib = d + 1 - 2 * lax.rem(d, 2)
    far_sib = lax.rem(sib + 2, n_dp)
    ins, outs = (rows_ref, grad_ref), (out_rows, out_grad)
    span = INNER * cap
    greet_all(n_dp, n_ctx)
    meta_src = lambda peer: meta_ref.at[0]

    def line_copy(a, j, up, first):
        return pltpu.make_async_remote_copy(
            src_ref=ins[a] if first else dense.at[a, j],
            dst_ref=dense.at[a, j],
            send_sem=line_send.at[a, int(up), j],
            recv_sem=line_recv.at[a, j],
            device_id=(d, (z + (1 if up else -1)) * INNER + y),
            device_id_type=MESH,
        )

    def relay(a, j, first, act):
        @pl.when((j <= z) & (z < length - 1))
        def _():
            act(line_copy(a, j, True, first))

        @pl.when((j >= z) & (z > 0))
        def _():
            act(line_copy(a, j, False, first))

    def meta_start(i, carry):
        spread_copy(n_dp, n_ctx, i, meta_src, meta_all, meta_send, meta_recv, True).start()
        return carry

    for a in range(2):
        relay(a, z, True, lambda copy: copy.start())
    lax.fori_loop(1, n, meta_start, 0)
    meta_all[pl.ds(me, 1)] = meta_ref[...]
    loads = [pltpu.make_async_copy(ins[a], dense.at[a, z], own_sem.at[a]) for a in range(2)]
    for load in loads:
        load.start()
    wloads = (
        pltpu.make_async_copy(wg_ref, pair_w.at[:, :, pl.ds(0, depth)], weight_sem.at[0]),
        pltpu.make_async_copy(wu_ref, pair_w.at[:, :, pl.ds(depth, depth)], weight_sem.at[1]),
        pltpu.make_async_copy(wd_ref, down_w, weight_sem.at[2]),
    )
    for load in wloads:
        load.start()

    def place(a, row, owner):
        slot = row * n_ctx + owner
        return outs[a].at[:, pl.ds(pl.multiple_of(slot * cap, 8), cap)]

    def forward(a, src, row, owner, to, send_sem, recv_sem):
        return pltpu.make_async_remote_copy(
            src_ref=src,
            dst_ref=place(a, row, owner),
            send_sem=send_sem,
            recv_sem=recv_sem,
            device_id=(to, c),
            device_id_type=MESH,
        )

    def near_copies(a, src, owner):
        return (
            forward(a, src, d, owner, far, far_send.at[a, owner], far_recv.at[a, owner]),
            forward(a, src, d, owner, sib, sib_send.at[a, 0, owner], sib_recv.at[a, 0, owner]),
        )

    def sib_copy(a, owner):
        src = place(a, far, owner)
        return forward(a, src, far, owner, sib, sib_send.at[a, 1, owner], sib_recv.at[a, 1, owner])

    def await_far(a, owner):
        row = place(a, far, owner)
        forward(a, row, far, owner, far, far_send.at[a, owner], far_recv.at[a, owner]).wait_recv()

    def await_sib(a, which, row, owner):
        src = place(a, row, owner)
        forward(
            a, src, row, owner, sib, sib_send.at[a, which, owner], sib_recv.at[a, which, owner]
        ).wait_recv()

    def side_copy(a, j, sending):
        return pltpu.make_async_remote_copy(
            src_ref=sel_side.at[a, j],
            dst_ref=place(a, d, j * INNER + (y if sending else 1 - y)),
            send_sem=side_send.at[a, j],
            recv_sem=side_recv.at[a, j],
            device_id=(d, side),
            device_id_type=MESH,
        )

    def own_store(a, j):
        return pltpu.make_async_copy(
            sel_own.at[a, j], place(a, d, j * INNER + y), store_sem.at[a, j]
        )

    def select(a, j):
        meta = meta_all[d * n_ctx + j * INNER + y]
        held = dense[a, j]
        for target, owner in ((sel_own, c), (sel_side, side)):
            for e in range(local):
                masks = slot_masks(meta, picks, cap, (owner * local + e) * cap)
                pick = sum(jnp.where(mask, 1.0, 0.0) for mask in masks).astype(jnp.bfloat16)
                target[a, j, e] = jnp.dot(
                    pick, held, preferred_element_type=jnp.float32
                ).astype(jnp.bfloat16)

    def emit(a, j):
        select(a, j)
        side_copy(a, j, True).start()
        owner = j * INNER + y
        for copy in near_copies(a, sel_own.at[a, j], owner):
            copy.start()
        own_store(a, j).start()

    def take_side(a, j):
        side_copy(a, j, False).wait_recv()
        owner = j * INNER + 1 - y
        for copy in near_copies(a, place(a, d, owner), owner):
            copy.start()

    def meta_wait(src):
        i = lax.rem(me + n - src, n)
        spread_copy(n_dp, n_ctx, i, meta_src, meta_all, meta_send, meta_recv, False).wait_recv()

    def segment(row, j):
        return pl.ds(pl.multiple_of((row * n_ctx + j * INNER) * cap, 8), span)

    def chunk_loads(rows, j):
        return [
            pltpu.make_async_copy(
                outs[a].at[:, segment(row, j)],
                chunk.at[a, :, pl.ds(i * span, span)],
                chunk_sem.at[a, i],
            )
            for a in range(2)
            for i, row in enumerate(rows)
        ]

    def chunk_stores(rows, j):
        return [
            pltpu.make_async_copy(
                held.at[:, pl.ds(i * span, span)], out.at[:, segment(row, j)], result_sem.at[b, i]
            )
            for b, (held, out) in enumerate(
                ((pair_out, out_pair), (hid_out, out_hid), (back_out, out_back))
            )
            for i, row in enumerate(rows)
        ]

    def compute(rows, j):
        for copy in chunk_loads(rows, j):
            copy.start()
        for copy in chunk_loads(rows, j):
            copy.wait()
        sources = [row * n_ctx + j * INNER + side_at for row in rows for side_at in range(INNER)]

        def expert(e, carry):
            masks = [
                slot_masks(meta_all[src], picks, cap, (c * local + e) * cap) for src in sources
            ]
            weight = jnp.concatenate(
                [
                    jnp.sum(
                        sum(
                            jnp.where(mask, meta_all[src, picks + k][None, :], 0.0)
                            for k, mask in enumerate(block)
                        ),
                        axis=1,
                        keepdims=True,
                    )
                    for src, block in zip(sources, masks)
                ],
                axis=0,
            )
            pre = jnp.dot(chunk[0, e], pair_w[e], preferred_element_type=jnp.float32)
            grad_out = lax.dot_general(
                chunk[1, e], down_w[e], (((1,), (1,)), ((), ())),
                preferred_element_type=jnp.float32,
            )
            gate_pre, up_pre = pre[:, :depth], pre[:, depth:]
            squash = jax.nn.sigmoid(SWISH_SCALE * gate_pre)
            swish = gate_pre * squash
            raised = up_pre + 1.0
            full = swish * raised
            hid_out[e] = (weight * full).astype(jnp.bfloat16)
            score = jnp.sum(
                grad_out * full.astype(jnp.bfloat16).astype(jnp.float32), axis=1, keepdims=True
            )
            grad_hidden = weight * grad_out
            slope = squash + SWISH_SCALE * swish * (1.0 - squash)
            pair_out[e, :, pl.ds(0, depth)] = (grad_hidden * raised * slope).astype(jnp.bfloat16)
            pair_out[e, :, pl.ds(depth, depth)] = (grad_hidden * swish).astype(jnp.bfloat16)
            back_out[e] = lax.dot_general(
                pair_out[e], pair_w[e], (((1,), (1,)), ((), ())),
                preferred_element_type=jnp.float32,
            ).astype(jnp.bfloat16)
            for i, (src, block) in enumerate(zip(sources, masks)):
                part = score[i * cap : (i + 1) * cap]
                lines = [
                    jnp.sum(jnp.where(mask, part, 0.0), axis=0, keepdims=True) for mask in block
                ]
                lines.append(jnp.zeros((picks, lines[0].shape[1]), jnp.float32))
                out_score[src] = out_score[src] + jnp.concatenate(lines, axis=0)
            return carry

        lax.fori_loop(0, local, expert, 0)
        for copy in chunk_stores(rows, j):
            copy.start()

    out_score[...] = jnp.zeros_like(out_score)
    for load in loads:
        load.wait()
    for a in range(2):
        emit(a, z)
    for load in wloads:
        load.wait()

    def line_meta(i, carry):
        src = d * n_ctx + lax.rem(z + i, length) * INNER + y
        meta_wait(src)
        return carry

    lax.fori_loop(1, length, line_meta, 0)

    def first_half(q):
        j = line_step(z, length, q)
        for a in range(2):
            own_store(a, j).wait()
            for side_at in range(INNER):
                await_sib(a, 0, sib, j * INNER + side_at)

        @pl.when(q > 0)
        def _():
            for copy in chunk_stores((d, sib), line_step(z, length, q - 1)):
                copy.wait()

        compute((d, sib), j)

    def outward(q, carry):
        j, before = line_step(z, length, q), line_step(z, length, q - 1)
        for a in range(2):
            line_copy(a, j, True, False).wait_recv()
            relay(a, j, False, lambda copy: copy.start())
            emit(a, j)
            take_side(a, before)

        @pl.when(q == 1)
        def _():
            lax.fori_loop(1, n, other_meta, 0)

        first_half(q - 1)
        return carry

    def other_meta(i, carry):
        src = lax.rem(me + n - i, n)
        inside = (lax.div(src, n_ctx) == d) & (lax.rem(src, INNER) == y)

        @pl.when(jnp.logical_not(inside))
        def _():
            meta_wait(src)

        return carry

    lax.fori_loop(1, length, outward, 0)
    last = line_step(z, length, length - 1)
    for a in range(2):
        take_side(a, last)
    first_half(length - 1)

    def inward(q, carry):
        j = line_step(z, length, q)
        for a in range(2):
            for owner in (j * INNER + y, j * INNER + 1 - y):
                await_far(a, owner)
                sib_copy(a, owner).start()
        for a in range(2):
            for owner in (j * INNER + y, j * INNER + 1 - y):
                await_sib(a, 1, far_sib, owner)

        @pl.when(q == 0)
        def _():
            for copy in chunk_stores((d, sib), last):
                copy.wait()

        @pl.when(q > 0)
        def _():
            for copy in chunk_stores((far, far_sib), line_step(z, length, q - 1)):
                copy.wait()

        compute((far, far_sib), j)
        return carry

    lax.fori_loop(0, length, inward, 0)
    for a in range(2):
        relay(a, z, True, lambda copy: copy.wait_send())

    def drain(q, carry):
        j = line_step(z, length, q)
        for a in range(2):

            @pl.when(q > 0)
            def _(a=a):
                relay(a, j, False, lambda copy: copy.wait_send())

            side_copy(a, j, True).wait_send()
            for owner in (j * INNER + y, j * INNER + 1 - y):
                for copy in near_copies(a, place(a, d, owner), owner):
                    copy.wait_send()
                sib_copy(a, owner).wait_send()
        return carry

    lax.fori_loop(0, length, drain, 0)

    def meta_finish(i, carry):
        spread_copy(n_dp, n_ctx, i, meta_src, meta_all, meta_send, meta_recv, True).wait_send()
        return carry

    lax.fori_loop(1, n, meta_finish, 0)
    for copy in chunk_stores((far, far_sib), last):
        copy.wait()


def dispatch_rows(rows, grad, meta, gate_weight, up_weight, down_weight, cap, n_dp, n_ctx):
    n = n_dp * n_ctx
    length = n_ctx // INNER
    tokens, width = rows.shape
    local, _, hidden = gate_weight.shape
    low = rows.dtype
    span = 2 * INNER * cap
    arrived = jax.ShapeDtypeStruct((local, n * cap, width), low)
    dma = pltpu.SemaphoreType.DMA
    return pl.pallas_call(
        functools.partial(dispatch_kernel, n_dp, n_ctx, cap),
        out_shape=(
            arrived,
            arrived,
            jax.ShapeDtypeStruct((local, n * cap, 2 * hidden), low),
            jax.ShapeDtypeStruct((local, n * cap, hidden), low),
            arrived,
            jax.ShapeDtypeStruct((n,) + meta.shape[1:], jnp.float32),
        ),
        in_specs=[ANY, ANY, VMEM, ANY, ANY, ANY],
        out_specs=(ANY,) * 5 + (VMEM,),
        scratch_shapes=[
            pltpu.VMEM((2, length, tokens, width), low),
            pltpu.VMEM((n,) + meta.shape[1:], jnp.float32),
            pltpu.VMEM((2, length, local, cap, width), low),
            pltpu.VMEM((2, length, local, cap, width), low),
            pltpu.VMEM((local, width, 2 * hidden), low),
            pltpu.VMEM(down_weight.shape, low),
            pltpu.VMEM((2, local, span, width), low),
            pltpu.VMEM((local, span, 2 * hidden), low),
            pltpu.VMEM((local, span, hidden), low),
            pltpu.VMEM((local, span, width), low),
            dma((n,)),
            dma((n,)),
            dma((2,)),
            dma((3,)),
            dma((2, 2, length)),
            dma((2, length)),
            dma((2, length)),
            dma((2, length)),
            dma((2, n_ctx)),
            dma((2, n_ctx)),
            dma((2, 2, n_ctx)),
            dma((2, 2, n_ctx)),
            dma((2, length)),
            dma((2, 2)),
            dma((3, 2)),
        ],
        compiler_params=pltpu.CompilerParams(
            collective_id=0, has_side_effects=True, vmem_limit_bytes=60 * 1024 * 1024
        ),
    )(rows, grad, meta, gate_weight, up_weight, down_weight)


def return_kernel(
    n_dp, n_ctx, cap, tile, back_ref, rows_ref, grad_ref, pair_ref, hid_ref, score_ref,
    out_ref, gate_out, up_out, down_out, out_score,
    mine, sib_land, far_out, far_land, done, pair, hid_raw, hid, row_tile, grad_tile, both, down,
    mine_sem, sib_send, sib_recv, far_send, far_recv, ring_send, ring_recv, own_sem,
    hold_sem, tile_sem, result_sem, score_send, score_recv,
):
    d, c = lax.axis_index("dp"), lax.axis_index("ctx")
    local = back_ref.shape[0]
    width, depth = rows_ref.shape[2], hid_ref.shape[2]
    across = width // tile
    units = local * across
    far = lax.rem(d + 2, n_dp)
    sib = d + 1 - 2 * lax.rem(d, 2)
    far_sib = lax.rem(sib + 2, n_dp)
    greet_all(n_dp, n_ctx)

    def dest(k):
        return lax.rem(c + k, n_ctx)

    def block(slot):
        return back_ref.at[:, pl.ds(pl.multiple_of(slot * cap, 8), cap)]

    def to_sib(k, which):
        row = far_sib if which == 0 else sib
        return pltpu.make_async_remote_copy(
            src_ref=block(row * n_ctx + dest(k)),
            dst_ref=sib_land.at[k, which],
            send_sem=sib_send.at[k, which],
            recv_sem=sib_recv.at[k, which],
            device_id=(sib, c),
            device_id_type=MESH,
        )

    def load(k, which):
        row = far if which == 0 else d
        return pltpu.make_async_copy(
            block(row * n_ctx + dest(k)), mine.at[k, which], mine_sem.at[k, which]
        )

    def to_far(k):
        return pltpu.make_async_remote_copy(
            src_ref=far_out.at[k],
            dst_ref=far_land.at[k],
            send_sem=far_send.at[k],
            recv_sem=far_recv.at[k],
            device_id=(far, c),
            device_id_type=MESH,
        )

    def ring(k, sending):
        owner = c if sending else lax.rem(c + n_ctx - k, n_ctx)
        return pltpu.make_async_remote_copy(
            src_ref=done.at[k],
            dst_ref=out_ref.at[owner],
            send_sem=ring_send.at[k],
            recv_sem=ring_recv.at[k],
            device_id=(d, dest(k)),
            device_id_type=MESH,
        )

    gaps = n_ctx + 1

    def turn(i):
        return lax.rem(i + 1, n_ctx)

    def tile_loads(u):
        e, slot = lax.div(u, across), lax.rem(u, 2)
        columns = pl.ds(pl.multiple_of(lax.rem(u, across) * tile, tile), tile)
        return (
            pltpu.make_async_copy(
                rows_ref.at[e, :, columns], row_tile.at[slot], tile_sem.at[0, slot]
            ),
            pltpu.make_async_copy(
                grad_ref.at[e, :, columns], grad_tile.at[slot], tile_sem.at[1, slot]
            ),
        )

    def results(u):
        e = lax.div(u, across)
        columns = pl.ds(pl.multiple_of(lax.rem(u, across) * tile, tile), tile)
        return (
            pltpu.make_async_copy(
                both.at[u, :, pl.ds(0, depth)], gate_out.at[e, columns], result_sem.at[0, u]
            ),
            pltpu.make_async_copy(
                both.at[u, :, pl.ds(depth, depth)], up_out.at[e, columns], result_sem.at[1, u]
            ),
            pltpu.make_async_copy(down.at[u], down_out.at[e, :, columns], result_sem.at[2, u]),
        )

    def unit(u, carry):
        for copy in tile_loads(u):
            copy.wait()

        @pl.when(u + 1 < units)
        def _():
            for copy in tile_loads(u + 1):
                copy.start()

        e, slot = lax.div(u, across), lax.rem(u, 2)
        both[u] = jnp.dot(
            row_tile[slot].T, pair[e], preferred_element_type=jnp.float32
        ).astype(jnp.bfloat16)
        down[u] = jnp.dot(
            hid[e], grad_tile[slot], preferred_element_type=jnp.float32
        ).astype(jnp.bfloat16)
        for copy in results(u):
            copy.start()
        return carry

    n = n_dp * n_ctx
    me = d * n_ctx + c
    score_src = lambda peer: score_ref.at[peer]

    def score_start(i, carry):
        spread_copy(n_dp, n_ctx, i, score_src, out_score, score_send, score_recv, True).start()
        return carry

    def score_finish(i, carry):
        spread_copy(n_dp, n_ctx, i, score_src, out_score, score_send, score_recv, True).wait_send()
        spread_copy(n_dp, n_ctx, i, score_src, out_score, score_send, score_recv, False).wait_recv()
        return carry

    def begin(i, carry):
        k = turn(i)
        for which in range(2):
            to_sib(k, which).start()
            load(k, which).start()
        return carry

    lax.fori_loop(0, n_ctx, begin, 0)
    holds = (
        pltpu.make_async_copy(pair_ref, pair, hold_sem.at[0]),
        pltpu.make_async_copy(hid_ref, hid_raw, hold_sem.at[1]),
    )
    for copy in holds:
        copy.start()
    for copy in tile_loads(0):
        copy.start()

    def outward(i, carry):
        k = turn(i)
        to_sib(k, 0).wait_recv()
        load(k, 0).wait()
        far_out[k] = (
            mine[k, 0].astype(jnp.float32) + sib_land[k, 0].astype(jnp.float32)
        ).astype(jnp.bfloat16)
        to_far(k).start()
        return carry

    lax.fori_loop(0, n_ctx, outward, 0)
    lax.fori_loop(1, n, score_start, 0)
    out_score[pl.ds(me, 1)] = score_ref[pl.ds(me, 1)]
    for copy in holds:
        copy.wait()
    for e in range(local):
        hid[e] = hid_raw[e].T

    def inward(i, carry):
        k = turn(i)
        lax.fori_loop(lax.div(i * units, gaps), lax.div((i + 1) * units, gaps), unit, 0)
        to_sib(k, 1).wait_recv()
        load(k, 1).wait()
        to_far(k).wait_recv()
        done[k] = (
            mine[k, 1].astype(jnp.float32)
            + sib_land[k, 1].astype(jnp.float32)
            + far_land[k].astype(jnp.float32)
        ).astype(jnp.bfloat16)

        @pl.when(k > 0)
        def _():
            ring(k, True).start()

        return carry

    lax.fori_loop(0, n_ctx, inward, 0)
    own = pltpu.make_async_copy(done.at[0], out_ref.at[c], own_sem)
    own.start()
    lax.fori_loop(n_ctx * units // gaps, units, unit, 0)
    own.wait()
    lax.fori_loop(1, n, score_finish, 0)

    def drain(k, carry):
        to_sib(k, 0).wait_send()
        to_sib(k, 1).wait_send()
        to_far(k).wait_send()

        @pl.when(k > 0)
        def _():
            ring(k, True).wait_send()
            ring(k, False).wait_recv()

        return carry

    lax.fori_loop(0, n_ctx, drain, 0)

    def store_wait(u, carry):
        for copy in results(u):
            copy.wait()
        return carry

    lax.fori_loop(0, units, store_wait, 0)


def return_rows(back, rows, grad, pair, hidden, score, n_dp, n_ctx):
    local, total, width = back.shape
    cap = total // (n_dp * n_ctx)
    depth = hidden.shape[2]
    tile = 256 if width % 256 == 0 else 128
    units = local * (width // tile)
    block = (local, cap, width)
    low = back.dtype
    return pl.pallas_call(
        functools.partial(return_kernel, n_dp, n_ctx, cap, tile),
        out_shape=(
            jax.ShapeDtypeStruct((n_ctx,) + block, low),
            jax.ShapeDtypeStruct((local, width, depth), low),
            jax.ShapeDtypeStruct((local, width, depth), low),
            jax.ShapeDtypeStruct((local, depth, width), low),
            jax.ShapeDtypeStruct(score.shape, jnp.float32),
        ),
        in_specs=[ANY] * 5 + [VMEM],
        out_specs=(ANY,) * 4 + (VMEM,),
        scratch_shapes=[
            pltpu.VMEM((n_ctx, 2) + block, low),
            pltpu.VMEM((n_ctx, 2) + block, low),
            pltpu.VMEM((n_ctx,) + block, low),
            pltpu.VMEM((n_ctx,) + block, low),
            pltpu.VMEM((n_ctx,) + block, low),
            pltpu.VMEM((local, total, 2 * depth), low),
            pltpu.VMEM((local, total, depth), low),
            pltpu.VMEM((local, depth, total), low),
            pltpu.VMEM((2, total, tile), low),
            pltpu.VMEM((2, total, tile), low),
            pltpu.VMEM((units, tile, 2 * depth), low),
            pltpu.VMEM((units, depth, tile), low),
            pltpu.SemaphoreType.DMA((n_ctx, 2)),
            pltpu.SemaphoreType.DMA((n_ctx, 2)),
            pltpu.SemaphoreType.DMA((n_ctx, 2)),
            pltpu.SemaphoreType.DMA((n_ctx,)),
            pltpu.SemaphoreType.DMA((n_ctx,)),
            pltpu.SemaphoreType.DMA((n_ctx,)),
            pltpu.SemaphoreType.DMA((n_ctx,)),
            pltpu.SemaphoreType.DMA,
            pltpu.SemaphoreType.DMA((2,)),
            pltpu.SemaphoreType.DMA((2, 2)),
            pltpu.SemaphoreType.DMA((3, units)),
            pltpu.SemaphoreType.DMA((n_dp * n_ctx,)),
            pltpu.SemaphoreType.DMA((n_dp * n_ctx,)),
        ],
        compiler_params=pltpu.CompilerParams(
            collective_id=1, has_side_effects=True, vmem_limit_bytes=60 * 1024 * 1024
        ),
    )(back, rows, grad, pair, hidden, score)


def tiles(x):
    return jnp.pad(x, ((0, 0), (0, 1024 - x.shape[1]))).reshape(x.shape[0], 8, 128)


def body(
    tokens, cotangent, expert_ids, norm_gain, router_weight, gate_weight, up_weight, down_weight
):
    n_ctx = lax.axis_size("ctx")
    n_dp = lax.axis_size("dp")
    n = n_dp * n_ctx
    local = gate_weight.shape[0]
    experts = router_weight.shape[1]
    rows_here = tokens.shape[0]
    picks = expert_ids.shape[1]
    width = tokens.shape[1]
    capacity = max(2, rows_here * picks * 5 // (4 * experts))
    capacity = -(-capacity // 8) * 8
    slots = experts * capacity
    widened = tokens.astype(jnp.float32)
    inverse = lax.rsqrt(jnp.mean(widened * widened, axis=1, keepdims=True) + EPSILON)
    scaled = widened * inverse
    normed = (scaled * norm_gain).astype(jnp.bfloat16)
    logits = jnp.dot(normed, router_weight, preferred_element_type=jnp.float32)
    labels = jnp.arange(experts, dtype=jnp.int32)
    member = expert_ids[:, :, None] == labels
    chosen = jnp.sum(jnp.where(member, logits[:, None, :], 0.0), axis=2)
    lifted = jnp.exp(chosen)
    gates = lifted / jnp.sum(lifted, axis=1, keepdims=True)
    hits = jnp.any(member, axis=1).astype(jnp.bfloat16)
    earlier = jnp.tril(jnp.ones((rows_here, rows_here), jnp.bfloat16), -1)
    count = jnp.dot(earlier, hits, preferred_element_type=jnp.float32)
    rank = jnp.sum(jnp.where(member, count[:, None, :], 0.0), axis=2)
    position = expert_ids.astype(jnp.float32) * capacity + rank
    meta = jnp.concatenate([position, gates], axis=1).T[None]
    rows, upstream, pair, hidden, back, score = dispatch_rows(
        normed, cotangent, meta, gate_weight, up_weight, down_weight, capacity, n_dp, n_ctx
    )
    back_slots, gate_grad, up_grad, down_grad, score_parts = return_rows(
        back, rows, upstream, pair, hidden, score, n_dp, n_ctx
    )
    score_tok = jnp.sum(score_parts, axis=0)[:picks].T
    back_flat = back_slots.reshape(slots, width)
    places = jnp.arange(slots, dtype=jnp.float32)[:, None]
    match = [places == position[:, k][None, :] for k in range(picks)]
    dispatch_low = sum(jnp.where(hit, 1.0, 0.0) for hit in match).astype(jnp.bfloat16)
    grad_tok = jnp.dot(dispatch_low.T, back_flat, preferred_element_type=jnp.float32)
    mixed = jnp.sum(gates * score_tok, axis=1, keepdims=True)
    grad_chosen = gates * (score_tok - mixed)
    grad_logits = jnp.sum(jnp.where(member, grad_chosen[:, :, None], 0.0), axis=1).astype(
        jnp.bfloat16
    )
    grad_normed = grad_tok + jnp.dot(
        grad_logits, router_weight.T, preferred_element_type=jnp.float32
    )
    router_part = jnp.dot(normed.T, grad_logits, preferred_element_type=jnp.float32)
    gain_part = jnp.sum(grad_normed * scaled, axis=0)
    share = width // n
    parts = jnp.concatenate(
        [router_part.reshape(n, share * experts), gain_part.reshape(n, share)], axis=1
    )
    sums = exchange(tiles(parts), n_dp, n_ctx, 1, 3).reshape(1024)
    router_grad = sums[: share * experts].reshape(share, experts)
    gain_grad = sums[share * experts : share * experts + share]
    grad_scaled = grad_normed * norm_gain
    correction = jnp.mean(grad_scaled * scaled, axis=1, keepdims=True)
    grad_input = (
        cotangent.astype(jnp.float32) + inverse * (grad_scaled - scaled * correction)
    ).astype(jnp.bfloat16)
    return (grad_input, gate_grad, up_grad, down_grad, router_grad, gain_grad)


def solution(mesh):
    return jax.shard_map(
        body,
        mesh=mesh,
        in_specs=(
            P(("dp", "ctx"), None),
            P(("dp", "ctx"), None),
            P(("dp", "ctx"), None),
            P(),
            P(),
            P("ctx", None, "dp"),
            P("ctx", None, "dp"),
            P("ctx", "dp", None),
        ),
        out_specs=(
            P(("dp", "ctx"), None),
            P("ctx", None, "dp"),
            P("ctx", None, "dp"),
            P("ctx", "dp", None),
            P(("dp", "ctx"), None),
            P(("dp", "ctx")),
        ),
        check_vma=False,
    )
```

time: 309 us -> 245 us (0.79)
  Pallas kernels: 250 us -> 222 us
  matrix products: 28.2 us -> 3.6 us
  other arithmetic: 14.3 us -> 6.45 us
    pallas_call x1, Pallas kernels: 92.9 us -> 68.7 us  [return_rows(): pl.pallas_call(functools.partial(return_kernel, n_dp, n_ctx, cap, tile),...]
    dot_general x5 -> x1, matrix products: 23.8 us -> 0.2 us  [body(): count = jnp.dot(earlier, hits, preferred_element_type=jnp.float32)]
    reduce_sum x5 -> x2, other arithmetic: 9.16 us -> 0.81 us  [the longest x1 0.77 us: body(): rank = jnp.sum(jnp.where(member, count[:, None, :], 0.0), axis=2)]
    pallas_call x1, Pallas kernels: 141 us -> 136 us  [dispatch_rows(): pl.pallas_call(functools.partial(dispatch_kernel, n_dp, n_ctx, cap), out_...]
    unnamed x32 -> x25, local copies, waits for them, and re-layouts: 11 us -> 9.45 us
where the time goes in v1:
time: 245 us; the launch traced here: 244 us
  Pallas kernels  222 us (91%)
  local copies, waits for them, and re-layouts  11.8 us (5%)
  other arithmetic  6.45 us (3%)
  matrix products  3.6 us (1%)
    pallas_call x1, Pallas kernels, dispatch_rows(): pl.pallas_call(functools.partial(dispatch_kernel, n_dp, n_ctx, cap), out_...  136 us
    pallas_call x1, Pallas kernels, return_rows(): pl.pallas_call(functools.partial(return_kernel, n_dp, n_ctx, cap, tile),...  68.7 us
    pallas_call x1, Pallas kernels, exchange(): pl.pallas_call(functools.partial(exchange_kernel, n_dp, n_ctx, keep), out...  16.4 us
    unnamed x25, local copies, waits for them, and re-layouts  9.45 us

profile of v1, /device:TPU:0, one launch (start us, length us, event | category | flops | bytes accessed | tf_op | source)
XLA Modules:
  0.0 244.1 jit_solution(734516360530465788)
XLA Ops:
  0.6 1.2 fusion.11
  1.9 0.7 fusion.24
  2.6 0.2 fusion.21
  2.8 1.2 fusion.4.rows_ref
  4.0 0.2 fusion.36
  4.2 0.8 select_reduce_fusion.2
  5.0 0.7 multiply_add_fusion
  5.7 0.6 maximum_bitcast_fusion.meta_ref
  6.3 136.4 %shard_map.127 = (bf16[2,1280,1792]{2,1,0:T(8,128)(2,1)}, bf16[2,1280,1792]{2,1,0:T(8,128)(2,1)}, bf16[2,1280,768]{2,1,0:T(8,128)(2,1)}, bf16[2,1280,384]{2,1,0:...) custom-call(bf16[128,1792]{1,0:T(8,128)(2,1)} %copy-done.2, bf16[128,1792]{1,0:T(8,128)(2,1)} %grad_ref.1, ...), custom_call_target="tpu_custom_call" | custom-call | tf_op jit(solution)/shard_map/pallas_call | solution.py:451
  142.7 68.7 %shard_map.128 = (bf16[8,2,40,1792]{3,2,1,0:T(8,128)(2,1)}, bf16[2,1792,384]{2,1,0:T(8,128)(2,1)}, bf16[2,1792,384]{2,1,0:T(8,128)(2,1)}, bf16[2,384,1792]{2,1,0:T(8,128)(2,1)}, f32[32,8,128]{2,1,0:T(8,128)}) custom-call(bf16[2,1280,1792]{2,1,0:T(8,128)(2,1)} %get-tuple-element.17.back_ref, bf16[2,1280,1792]{2,1,0:T(8,128)(2,1)} %get-tuple-element.18.rows_ref, ...), custom_call_target="tpu_custom_call" | custom-call | tf_op jit(solution)/shard_map/pallas_call | solution.py:710
  211.4 2.4 fusion.12
  213.9 0.5 fusion.10
  214.5 1.1 fusion.9
  215.7 0.3 fusion.37
  216.0 0.3 reshape.56
  216.3 0.7 copy.28
  217.0 16.4 %shard_map.129 = f32[1,8,128]{2,1,0:T(8,128)} custom-call(f32[32,8,128]{2,1,0:T(8,128)} %bitcast.34), custom_call_target="tpu_custom_call" | custom-call | tf_op jit(solution)/shard_map/pallas_call | solution.py:76
  233.5 1.2 slice.28
  234.7 0.8 reshape.59
  235.4 0.7 copy.26
  236.1 3.7 %copy.32 = bf16[2,1792,384]{2,1,0:T(8,128)(2,1)} copy(bf16[2,1792,384]{2,1,0:T(8,128)(2,1)} %get-tuple-element.64) | data formatting | bytes 5505024
  239.8 1.5 copy.33
  241.4 1.2 copy-done.4
  242.6 1.5 copy.34
  (30 shorter events, 0.3 us)
Async XLA Ops:
  0.6 3.4 %copy-start = (bf16[1792,16]{0,1:T(8,128)(2,1)S(1)}, bf16[1792,16]{0,1:T(8,128)(2,1)}, u32[]{:S(2)}) copy-start(bf16[1792,16]{0,1:T(8,128)(2,1)} %param.12) | copy-start | bytes 172036
  4.0 2.3 copy-start.2
  211.4 2.4 copy-start.7
  211.4 2.5 %copy-start.9 = (s32[128,4]{0,1:T(4,128)S(1)}, s32[128,4]{0,1:T(4,128)}, u32[]{:S(2)}) copy-start(s32[128,4]{0,1:T(4,128)} %param.10) | copy-start | bytes 6148
  211.4 2.5 %copy-start.1 = (bf16[128,1792]{1,0:T(8,128)(2,1)S(1)}, bf16[128,1792]{1,0:T(8,128)(2,1)}, u32[]{:S(2)}) copy-start(bf16[128,1792]{1,0:T(8,128)(2,1)} %param.8) | copy-start | bytes 1376260
  211.4 2.5 %copy-start.8 = (f32[1792]{0:T(1024)S(1)}, f32[1792]{0:T(1024)}, u32[]{:S(2)}) copy-start(f32[1792]{0:T(1024)} %param.11) | copy-start | bytes 21508
  211.4 3.1 %copy-start.6 = (bf16[128,1792]{1,0:T(8,128)(2,1)S(1)}, bf16[128,1792]{1,0:T(8,128)(2,1)}, u32[]{:S(2)}) copy-start(bf16[128,1792]{1,0:T(8,128)(2,1)} %grad_ref.1) | copy-start | bytes 1376260
  213.8 1.9 copy-start.3
  236.1 3.7 %copy-start.5 = (bf16[2,1792,384]{2,1,0:T(8,128)(2,1)S(1)}, bf16[2,1792,384]{2,1,0:T(8,128)(2,1)}, u32[]{:S(2)}) copy-start(bf16[2,1792,384]{2,1,0:T(8,128)(2,1)} %get-tuple-element.65) | copy-start | bytes 8257540
  239.8 2.8 %copy-start.4 = (bf16[2,384,1792]{2,1,0:T(8,128)(2,1)S(1)}, bf16[2,384,1792]{2,1,0:T(8,128)(2,1)}, u32[]{:S(2)}) copy-start(bf16[2,384,1792]{2,1,0:T(8,128)(2,1)} %get-tuple-element.66) | copy-start | bytes 8257540

commit v2 on v1

--- a/solution.py
+++ b/solution.py
@@ -105,10 +105,11 @@
 
 def dispatch_kernel(
     n_dp, n_ctx, cap, rows_ref, grad_ref, meta_ref, wg_ref, wu_ref, wd_ref,
-    out_rows, out_grad, out_pair, out_hid, out_back, out_score,
-    dense, meta_all, sel_own, sel_side, pair_w, down_w, chunk, pair_out, hid_out, back_out,
+    out_rows, out_grad, out_pair, out_hid, out_back, out_score, meta_all,
+    dense, sel_own, sel_side, pair_w, down_w, chunk, pair_out, hid_out, back_out,
     meta_send, meta_recv, own_sem, weight_sem, line_send, line_recv, side_send, side_recv,
     far_send, far_recv, sib_send, sib_recv, store_sem, chunk_sem, result_sem,
+    cross_send, cross_recv,
 ):
     n = n_dp * n_ctx
     local, depth = wd_ref.shape[0], wd_ref.shape[1]
@@ -120,6 +121,8 @@
     far = lax.rem(d + 2, n_dp)
     sib = d + 1 - 2 * lax.rem(d, 2)
     far_sib = lax.rem(sib + 2, n_dp)
+    core = lax.rem(d, 2)
+    streams = ((0, d, 0), (1, d, 0), (1, far, 1))
     ins, outs = (rows_ref, grad_ref), (out_rows, out_grad)
     span = INNER * cap
     greet_all(n_dp, n_ctx)
@@ -148,9 +151,24 @@
         spread_copy(n_dp, n_ctx, i, meta_src, meta_all, meta_send, meta_recv, True).start()
         return carry
 
+    def on_core(s, act):
+        if s == 2:
+            pl.when(core == 0)(act)
+        else:
+            act()
+
+    cross = pltpu.make_async_remote_copy(
+        src_ref=grad_ref,
+        dst_ref=dense.at[2, z],
+        send_sem=cross_send,
+        recv_sem=cross_recv,
+        device_id=(far, c),
+        device_id_type=MESH,
+    )
+    lax.fori_loop(1, n, meta_start, 0)
+    pl.when(core == 0)(lambda: cross.start())
     for a in range(2):
         relay(a, z, True, lambda copy: copy.start())
-    lax.fori_loop(1, n, meta_start, 0)
     meta_all[pl.ds(me, 1)] = meta_ref[...]
     loads = [pltpu.make_async_copy(ins[a], dense.at[a, z], own_sem.at[a]) for a in range(2)]
     for load in loads:
@@ -177,11 +195,17 @@
             device_id_type=MESH,
         )
 
-    def near_copies(a, src, owner):
-        return (
-            forward(a, src, d, owner, far, far_send.at[a, owner], far_recv.at[a, owner]),
-            forward(a, src, d, owner, sib, sib_send.at[a, 0, owner], sib_recv.at[a, 0, owner]),
-        )
+    def near_copies(s, src, owner, act):
+        a, row, which = streams[s]
+        to_far = lambda: act(
+            forward(a, src, row, owner, far, far_send.at[a, owner], far_recv.at[a, owner])
+        )
+        if s == 0:
+            to_far()
+        if s == 1:
+            pl.when(core == 1)(to_far)
+        send, recv = sib_send.at[a, which, owner], sib_recv.at[a, which, owner]
+        act(forward(a, src, row, owner, sib, send, recv))
 
     def sib_copy(a, owner):
         src = place(a, far, owner)
@@ -197,68 +221,65 @@
             a, src, row, owner, sib, sib_send.at[a, which, owner], sib_recv.at[a, which, owner]
         ).wait_recv()
 
-    def side_copy(a, j, sending):
+    def side_copy(s, j, sending):
+        a, row, _ = streams[s]
         return pltpu.make_async_remote_copy(
-            src_ref=sel_side.at[a, j],
-            dst_ref=place(a, d, j * INNER + (y if sending else 1 - y)),
-            send_sem=side_send.at[a, j],
-            recv_sem=side_recv.at[a, j],
+            src_ref=sel_side.at[s, j],
+            dst_ref=place(a, row, j * INNER + (y if sending else 1 - y)),
+            send_sem=side_send.at[s, j],
+            recv_sem=side_recv.at[s, j],
             device_id=(d, side),
             device_id_type=MESH,
         )
 
-    def own_store(a, j):
+    def own_store(s, j):
+        a, row, _ = streams[s]
         return pltpu.make_async_copy(
-            sel_own.at[a, j], place(a, d, j * INNER + y), store_sem.at[a, j]
-        )
-
-    def select(a, j):
-        meta = meta_all[d * n_ctx + j * INNER + y]
-        held = dense[a, j]
+            sel_own.at[s, j], place(a, row, j * INNER + y), store_sem.at[s, j]
+        )
+
+    def select(s, j):
+        meta = meta_all[streams[s][1] * n_ctx + j * INNER + y]
+        held = dense[s, j]
         for target, owner in ((sel_own, c), (sel_side, side)):
             for e in range(local):
                 masks = slot_masks(meta, picks, cap, (owner * local + e) * cap)
                 pick = sum(jnp.where(mask, 1.0, 0.0) for mask in masks).astype(jnp.bfloat16)
-                target[a, j, e] = jnp.dot(
+                target[s, j, e] = jnp.dot(
                     pick, held, preferred_element_type=jnp.float32
                 ).astype(jnp.bfloat16)
 
-    def emit(a, j):
-        select(a, j)
-        side_copy(a, j, True).start()
-        owner = j * INNER + y
-        for copy in near_copies(a, sel_own.at[a, j], owner):
-            copy.start()
-        own_store(a, j).start()
-
-    def take_side(a, j):
-        side_copy(a, j, False).wait_recv()
+    def emit(s, j):
+        select(s, j)
+        side_copy(s, j, True).start()
+        near_copies(s, sel_own.at[s, j], j * INNER + y, lambda copy: copy.start())
+        own_store(s, j).start()
+
+    def take_side(s, j):
+        side_copy(s, j, False).wait_recv()
+        a, row, _ = streams[s]
         owner = j * INNER + 1 - y
-        for copy in near_copies(a, place(a, d, owner), owner):
-            copy.start()
-
-    def meta_wait(src):
-        i = lax.rem(me + n - src, n)
-        spread_copy(n_dp, n_ctx, i, meta_src, meta_all, meta_send, meta_recv, False).wait_recv()
+        near_copies(s, place(a, row, owner), owner, lambda copy: copy.start())
 
     def segment(row, j):
         return pl.ds(pl.multiple_of((row * n_ctx + j * INNER) * cap, 8), span)
 
-    def chunk_loads(rows, j):
+    def chunk_loads(half, i, row, j):
         return [
             pltpu.make_async_copy(
                 outs[a].at[:, segment(row, j)],
-                chunk.at[a, :, pl.ds(i * span, span)],
-                chunk_sem.at[a, i],
+                chunk.at[half, a, :, pl.ds(i * span, span)],
+                chunk_sem.at[half, a, i],
             )
             for a in range(2)
-            for i, row in enumerate(rows)
         ]
 
-    def chunk_stores(rows, j):
+    def chunk_stores(half, rows, j):
         return [
             pltpu.make_async_copy(
-                held.at[:, pl.ds(i * span, span)], out.at[:, segment(row, j)], result_sem.at[b, i]
+                held.at[half, :, pl.ds(i * span, span)],
+                out.at[:, segment(row, j)],
+                result_sem.at[half, b, i],
             )
             for b, (held, out) in enumerate(
                 ((pair_out, out_pair), (hid_out, out_hid), (back_out, out_back))
@@ -266,11 +287,16 @@
             for i, row in enumerate(rows)
         ]
 
-    def compute(rows, j):
-        for copy in chunk_loads(rows, j):
-            copy.start()
-        for copy in chunk_loads(rows, j):
-            copy.wait()
+    def compute(half, rows, j):
+        for i, row in enumerate(rows):
+            for copy in chunk_loads(half, i, row, j):
+                copy.wait()
+
+        @pl.when(j != z)
+        def _():
+            for copy in chunk_stores(half, rows, j):
+                copy.wait()
+
         sources = [row * n_ctx + j * INNER + side_at for row in rows for side_at in range(INNER)]
 
         def expert(e, carry):
@@ -291,9 +317,9 @@
                 ],
                 axis=0,
             )
-            pre = jnp.dot(chunk[0, e], pair_w[e], preferred_element_type=jnp.float32)
+            pre = jnp.dot(chunk[half, 0, e], pair_w[e], preferred_element_type=jnp.float32)
             grad_out = lax.dot_general(
-                chunk[1, e], down_w[e], (((1,), (1,)), ((), ())),
+                chunk[half, 1, e], down_w[e], (((1,), (1,)), ((), ())),
                 preferred_element_type=jnp.float32,
             )
             gate_pre, up_pre = pre[:, :depth], pre[:, depth:]
@@ -301,16 +327,16 @@
             swish = gate_pre * squash
             raised = up_pre + 1.0
             full = swish * raised
-            hid_out[e] = (weight * full).astype(jnp.bfloat16)
+            hid_out[half, e] = (weight * full).astype(jnp.bfloat16)
             score = jnp.sum(
                 grad_out * full.astype(jnp.bfloat16).astype(jnp.float32), axis=1, keepdims=True
             )
             grad_hidden = weight * grad_out
             slope = squash + SWISH_SCALE * swish * (1.0 - squash)
-            pair_out[e, :, pl.ds(0, depth)] = (grad_hidden * raised * slope).astype(jnp.bfloat16)
-            pair_out[e, :, pl.ds(depth, depth)] = (grad_hidden * swish).astype(jnp.bfloat16)
-            back_out[e] = lax.dot_general(
-                pair_out[e], pair_w[e], (((1,), (1,)), ((), ())),
+            pair_out[half, e, :, pl.ds(0, depth)] = (grad_hidden * raised * slope).astype(jnp.bfloat16)
+            pair_out[half, e, :, pl.ds(depth, depth)] = (grad_hidden * swish).astype(jnp.bfloat16)
+            back_out[half, e] = lax.dot_general(
+                pair_out[half, e], pair_w[e], (((1,), (1,)), ((), ())),
                 preferred_element_type=jnp.float32,
             ).astype(jnp.bfloat16)
             for i, (src, block) in enumerate(zip(sources, masks)):
@@ -323,7 +349,7 @@
             return carry
 
         lax.fori_loop(0, local, expert, 0)
-        for copy in chunk_stores(rows, j):
+        for copy in chunk_stores(half, rows, j):
             copy.start()
 
     out_score[...] = jnp.zeros_like(out_score)
@@ -334,109 +360,124 @@
     for load in wloads:
         load.wait()
 
-    def line_meta(i, carry):
-        src = d * n_ctx + lax.rem(z + i, length) * INNER + y
-        meta_wait(src)
-        return carry
-
-    lax.fori_loop(1, length, line_meta, 0)
-
-    def first_half(q):
-        j = line_step(z, length, q)
-        for a in range(2):
-            own_store(a, j).wait()
-            for side_at in range(INNER):
-                await_sib(a, 0, sib, j * INNER + side_at)
-
-        @pl.when(q > 0)
-        def _():
-            for copy in chunk_stores((d, sib), line_step(z, length, q - 1)):
-                copy.wait()
-
-        compute((d, sib), j)
-
-    def outward(q, carry):
-        j, before = line_step(z, length, q), line_step(z, length, q - 1)
-        for a in range(2):
-            line_copy(a, j, True, False).wait_recv()
-            relay(a, j, False, lambda copy: copy.start())
-            emit(a, j)
-            take_side(a, before)
-
-        @pl.when(q == 1)
-        def _():
-            lax.fori_loop(1, n, other_meta, 0)
-
-        first_half(q - 1)
-        return carry
-
-    def other_meta(i, carry):
-        src = lax.rem(me + n - i, n)
-        inside = (lax.div(src, n_ctx) == d) & (lax.rem(src, INNER) == y)
-
-        @pl.when(jnp.logical_not(inside))
-        def _():
-            meta_wait(src)
-
-        return carry
-
-    lax.fori_loop(1, length, outward, 0)
-    last = line_step(z, length, length - 1)
-    for a in range(2):
-        take_side(a, last)
-    first_half(length - 1)
-
-    def inward(q, carry):
-        j = line_step(z, length, q)
-        for a in range(2):
+    def meta_arrival(i, carry):
+        spread_copy(n_dp, n_ctx, i, meta_src, meta_all, meta_send, meta_recv, False).wait_recv()
+        return carry
+
+    lax.fori_loop(1, n, meta_arrival, 0)
+
+    @pl.when(core == 0)
+    def _():
+        cross.wait_recv()
+        relay(2, z, False, lambda copy: copy.start())
+        emit(2, z)
+
+    def each(r, act):
+        def step(k, carry):
+            j = z + (2 * k - 1) * r
+            pl.when((j >= 0) & (j < length) & (r + k > 0))(lambda: act(j))
+            return carry
+
+        lax.fori_loop(0, 2, step, 0)
+
+    def pass_far(j):
+        def one(a):
             for owner in (j * INNER + y, j * INNER + 1 - y):
                 await_far(a, owner)
                 sib_copy(a, owner).start()
+
+        one(0)
+        pl.when(core == 1)(lambda: one(1))
+
+    def first_half(j):
+        for a in range(2):
+            own_store(a, j).wait()
+        for copy in chunk_loads(0, 0, d, j):
+            copy.start()
+        for a in range(2):
+            for side_at in range(INNER):
+                await_sib(a, 0, sib, j * INNER + side_at)
+        for copy in chunk_loads(0, 1, sib, j):
+            copy.start()
+        compute(0, (d, sib), j)
+
+    def second_half(j):
+        pass_far(j)
+        pl.when(core == 0)(lambda: own_store(2, j).wait())
+        for copy in chunk_loads(1, 0, far, j):
+            copy.start()
         for a in range(2):
             for owner in (j * INNER + y, j * INNER + 1 - y):
                 await_sib(a, 1, far_sib, owner)
-
-        @pl.when(q == 0)
+        for copy in chunk_loads(1, 1, far_sib, j):
+            copy.start()
+        compute(1, (far, far_sib), j)
+
+    def arrive(s, j):
+        line_copy(s, j, True, False).wait_recv()
+        relay(s, j, False, lambda copy: copy.start())
+        emit(s, j)
+
+    def take_last(r):
+        pl.when(core == 0)(lambda: each(r, lambda j: take_side(2, j)))
+        pl.when(core == 1)(lambda: each(r, lambda j: take_side(1, j)))
+
+    def outward(r, carry):
+        ready = line_step(z, length, r - 1)
+        each(r, lambda j: arrive(0, j))
+        take_last(r - 1)
+        first_half(ready)
+        each(r, lambda j: arrive(1, j))
+        each(r, lambda j: take_side(0, j))
+        second_half(ready)
+
+        @pl.when(core == 0)
         def _():
-            for copy in chunk_stores((d, sib), last):
-                copy.wait()
-
-        @pl.when(q > 0)
-        def _():
-            for copy in chunk_stores((far, far_sib), line_step(z, length, q - 1)):
-                copy.wait()
-
-        compute((far, far_sib), j)
-        return carry
-
-    lax.fori_loop(0, length, inward, 0)
+            each(r, lambda j: arrive(2, j))
+            each(r, lambda j: take_side(1, j))
+
+        return carry
+
+    take_side(0, z)
+    pl.when(core == 0)(lambda: take_side(1, z))
+    lax.fori_loop(1, length, outward, 0)
+    take_last(length - 1)
+    final = line_step(z, length, length - 1)
+    first_half(final)
+    second_half(final)
+    for half, rows in enumerate(((d, sib), (far, far_sib))):
+        for copy in chunk_stores(half, rows, z):
+            copy.wait()
     for a in range(2):
         relay(a, z, True, lambda copy: copy.wait_send())
 
-    def drain(q, carry):
-        j = line_step(z, length, q)
-        for a in range(2):
-
-            @pl.when(q > 0)
-            def _(a=a):
-                relay(a, j, False, lambda copy: copy.wait_send())
-
-            side_copy(a, j, True).wait_send()
-            for owner in (j * INNER + y, j * INNER + 1 - y):
-                for copy in near_copies(a, place(a, d, owner), owner):
-                    copy.wait_send()
-                sib_copy(a, owner).wait_send()
+    def drain(j, carry):
+        for s in range(3):
+
+            def settle(s=s):
+                a, row, _ = streams[s]
+                if s < 2:
+                    pl.when(j != z)(lambda: relay(s, j, False, lambda copy: copy.wait_send()))
+                else:
+                    relay(s, j, False, lambda copy: copy.wait_send())
+                side_copy(s, j, True).wait_send()
+                for owner in (j * INNER + y, j * INNER + 1 - y):
+                    near_copies(s, place(a, row, owner), owner, lambda copy: copy.wait_send())
+
+            on_core(s, settle)
+        for owner in (j * INNER + y, j * INNER + 1 - y):
+            sib_copy(0, owner).wait_send()
+            pl.when(core == 1)(lambda owner=owner: sib_copy(1, owner).wait_send())
         return carry
 
     lax.fori_loop(0, length, drain, 0)
+    pl.when(core == 0)(lambda: cross.wait_send())
 
     def meta_finish(i, carry):
         spread_copy(n_dp, n_ctx, i, meta_src, meta_all, meta_send, meta_recv, True).wait_send()
         return carry
 
     lax.fori_loop(1, n, meta_finish, 0)
-    for copy in chunk_stores((far, far_sib), last):
-        copy.wait()
 
 
 def dispatch_rows(rows, grad, meta, gate_weight, up_weight, down_weight, cap, n_dp, n_ctx):
@@ -457,35 +498,37 @@
             jax.ShapeDtypeStruct((local, n * cap, hidden), low),
             arrived,
             jax.ShapeDtypeStruct((n,) + meta.shape[1:], jnp.float32),
+            jax.ShapeDtypeStruct((n,) + meta.shape[1:], jnp.float32),
         ),
         in_specs=[ANY, ANY, VMEM, ANY, ANY, ANY],
-        out_specs=(ANY,) * 5 + (VMEM,),
+        out_specs=(ANY,) * 5 + (VMEM,) * 2,
         scratch_shapes=[
-            pltpu.VMEM((2, length, tokens, width), low),
-            pltpu.VMEM((n,) + meta.shape[1:], jnp.float32),
-            pltpu.VMEM((2, length, local, cap, width), low),
-            pltpu.VMEM((2, length, local, cap, width), low),
+            pltpu.VMEM((3, length, tokens, width), low),
+            pltpu.VMEM((3, length, local, cap, width), low),
+            pltpu.VMEM((3, length, local, cap, width), low),
             pltpu.VMEM((local, width, 2 * hidden), low),
             pltpu.VMEM(down_weight.shape, low),
+            pltpu.VMEM((2, 2, local, span, width), low),
+            pltpu.VMEM((2, local, span, 2 * hidden), low),
+            pltpu.VMEM((2, local, span, hidden), low),
             pltpu.VMEM((2, local, span, width), low),
-            pltpu.VMEM((local, span, 2 * hidden), low),
-            pltpu.VMEM((local, span, hidden), low),
-            pltpu.VMEM((local, span, width), low),
             dma((n,)),
             dma((n,)),
             dma((2,)),
             dma((3,)),
-            dma((2, 2, length)),
-            dma((2, length)),
-            dma((2, length)),
-            dma((2, length)),
+            dma((3, 2, length)),
+            dma((3, length)),
+            dma((3, length)),
+            dma((3, length)),
             dma((2, n_ctx)),
             dma((2, n_ctx)),
             dma((2, 2, n_ctx)),
             dma((2, 2, n_ctx)),
-            dma((2, length)),
-            dma((2, 2)),
-            dma((3, 2)),
+            dma((3, length)),
+            dma((2, 2, 2)),
+            dma((2, 3, 2)),
+            dma,
+            dma,
         ],
         compiler_params=pltpu.CompilerParams(
             collective_id=0, has_side_effects=True, vmem_limit_bytes=60 * 1024 * 1024
@@ -494,70 +537,91 @@
 
 
 def return_kernel(
-    n_dp, n_ctx, cap, tile, back_ref, rows_ref, grad_ref, pair_ref, hid_ref, score_ref,
-    out_ref, gate_out, up_out, down_out, out_score,
-    mine, sib_land, far_out, far_land, done, pair, hid_raw, hid, row_tile, grad_tile, both, down,
-    mine_sem, sib_send, sib_recv, far_send, far_recv, ring_send, ring_recv, own_sem,
-    hold_sem, tile_sem, result_sem, score_send, score_recv,
+    n_dp, n_ctx, cap, tile, back_ref, rows_ref, grad_ref, pair_ref, hid_ref, score_ref, meta_ref,
+    gate_out, up_out, down_out, out_score, out_tok,
+    mine, sib_land, far_land, side_land, running, land, pair, hid_raw, hid, row_tile, grad_tile,
+    both, down, mine_sem, sib_send, sib_recv, far_send, far_recv, side_send, side_recv,
+    line_send, line_recv, hold_sem, tile_sem, result_sem, score_send, score_recv,
 ):
     d, c = lax.axis_index("dp"), lax.axis_index("ctx")
+    z, y, length = line_of(c, n_ctx)
     local = back_ref.shape[0]
+    picks = meta_ref.shape[1] // 2
     width, depth = rows_ref.shape[2], hid_ref.shape[2]
     across = width // tile
     units = local * across
+    side = z * INNER + 1 - y
     far = lax.rem(d + 2, n_dp)
     sib = d + 1 - 2 * lax.rem(d, 2)
     far_sib = lax.rem(sib + 2, n_dp)
     greet_all(n_dp, n_ctx)
 
-    def dest(k):
-        return lax.rem(c + k, n_ctx)
-
     def block(slot):
         return back_ref.at[:, pl.ds(pl.multiple_of(slot * cap, 8), cap)]
 
-    def to_sib(k, which):
+    def to_sib(owner, which):
         row = far_sib if which == 0 else sib
         return pltpu.make_async_remote_copy(
-            src_ref=block(row * n_ctx + dest(k)),
-            dst_ref=sib_land.at[k, which],
-            send_sem=sib_send.at[k, which],
-            recv_sem=sib_recv.at[k, which],
+            src_ref=block(row * n_ctx + owner),
+            dst_ref=sib_land.at[owner, which],
+            send_sem=sib_send.at[owner, which],
+            recv_sem=sib_recv.at[owner, which],
             device_id=(sib, c),
             device_id_type=MESH,
         )
 
-    def load(k, which):
+    def load(owner, which):
         row = far if which == 0 else d
         return pltpu.make_async_copy(
-            block(row * n_ctx + dest(k)), mine.at[k, which], mine_sem.at[k, which]
-        )
-
-    def to_far(k):
+            block(row * n_ctx + owner), mine.at[owner, which], mine_sem.at[owner, which]
+        )
+
+    def to_far(owner):
         return pltpu.make_async_remote_copy(
-            src_ref=far_out.at[k],
-            dst_ref=far_land.at[k],
-            send_sem=far_send.at[k],
-            recv_sem=far_recv.at[k],
+            src_ref=mine.at[owner, 0],
+            dst_ref=far_land.at[owner],
+            send_sem=far_send.at[owner],
+            recv_sem=far_recv.at[owner],
             device_id=(far, c),
             device_id_type=MESH,
         )
 
-    def ring(k, sending):
-        owner = c if sending else lax.rem(c + n_ctx - k, n_ctx)
+    def to_side(j):
         return pltpu.make_async_remote_copy(
-            src_ref=done.at[k],
-            dst_ref=out_ref.at[owner],
-            send_sem=ring_send.at[k],
-            recv_sem=ring_recv.at[k],
-            device_id=(d, dest(k)),
+            src_ref=mine.at[j * INNER + 1 - y, 1],
+            dst_ref=side_land.at[j],
+            send_sem=side_send.at[j],
+            recv_sem=side_recv.at[j],
+            device_id=(d, side),
             device_id_type=MESH,
         )
 
-    gaps = n_ctx + 1
-
-    def turn(i):
-        return lax.rem(i + 1, n_ctx)
+    def along(j, up, slot):
+        return pltpu.make_async_remote_copy(
+            src_ref=running.at[j],
+            dst_ref=land.at[slot],
+            send_sem=line_send.at[j],
+            recv_sem=line_recv.at[slot],
+            device_id=(d, (z + (1 if up else -1)) * INNER + y),
+            device_id_type=MESH,
+        )
+
+    def pass_on(j, act):
+        pl.when(j > z)(lambda: act(along(j, True, j)))
+        pl.when((j < z) & (j < z - 1))(lambda: act(along(j, False, j)))
+        pl.when((j < z) & (j == z - 1))(lambda: act(along(j, False, length)))
+
+    def each(r, act):
+        for k in range(2):
+            j = z + (2 * k - 1) * r
+            pl.when((j >= 0) & (j < length) & (r + k > 0))(lambda j=j: act(j))
+
+    def outermost(act):
+        def step(i, carry):
+            each(length - 1 - i, act)
+            return carry
+
+        lax.fori_loop(0, length, step, 0)
 
     def tile_loads(u):
         e, slot = lax.div(u, across), lax.rem(u, 2)
@@ -617,14 +681,13 @@
         spread_copy(n_dp, n_ctx, i, score_src, out_score, score_send, score_recv, False).wait_recv()
         return carry
 
-    def begin(i, carry):
-        k = turn(i)
-        for which in range(2):
-            to_sib(k, which).start()
-            load(k, which).start()
-        return carry
-
-    lax.fori_loop(0, n_ctx, begin, 0)
+    def begin(j, which):
+        for at in range(INNER):
+            to_sib(j * INNER + at, which).start()
+            load(j * INNER + at, which).start()
+
+    for which in range(2):
+        outermost(lambda j, which=which: begin(j, which))
     holds = (
         pltpu.make_async_copy(pair_ref, pair, hold_sem.at[0]),
         pltpu.make_async_copy(hid_ref, hid_raw, hold_sem.at[1]),
@@ -634,17 +697,19 @@
     for copy in tile_loads(0):
         copy.start()
 
-    def outward(i, carry):
-        k = turn(i)
-        to_sib(k, 0).wait_recv()
-        load(k, 0).wait()
-        far_out[k] = (
-            mine[k, 0].astype(jnp.float32) + sib_land[k, 0].astype(jnp.float32)
-        ).astype(jnp.bfloat16)
-        to_far(k).start()
-        return carry
-
-    lax.fori_loop(0, n_ctx, outward, 0)
+    def widen(value):
+        return value.astype(jnp.float32)
+
+    def outward(j):
+        for owner in (j * INNER + 1 - y, j * INNER + y):
+            to_sib(owner, 0).wait_recv()
+            load(owner, 0).wait()
+            mine[owner, 0] = (widen(mine[owner, 0]) + widen(sib_land[owner, 0])).astype(
+                jnp.bfloat16
+            )
+            to_far(owner).start()
+
+    outermost(outward)
     lax.fori_loop(1, n, score_start, 0)
     out_score[pl.ds(me, 1)] = score_ref[pl.ds(me, 1)]
     for copy in holds:
@@ -652,44 +717,80 @@
     for e in range(local):
         hid[e] = hid_raw[e].T
 
-    def inward(i, carry):
-        k = turn(i)
-        lax.fori_loop(lax.div(i * units, gaps), lax.div((i + 1) * units, gaps), unit, 0)
-        to_sib(k, 1).wait_recv()
-        load(k, 1).wait()
-        to_far(k).wait_recv()
-        done[k] = (
-            mine[k, 1].astype(jnp.float32)
-            + sib_land[k, 1].astype(jnp.float32)
-            + far_land[k].astype(jnp.float32)
-        ).astype(jnp.bfloat16)
-
-        @pl.when(k > 0)
+    def inward(j):
+        for owner in (j * INNER + 1 - y, j * INNER + y):
+            to_sib(owner, 1).wait_recv()
+            load(owner, 1).wait()
+            to_far(owner).wait_recv()
+            mine[owner, 1] = (
+                widen(mine[owner, 1]) + widen(sib_land[owner, 1]) + widen(far_land[owner])
+            ).astype(jnp.bfloat16)
+        to_side(j).start()
+
+    def spread(j):
+        to_side(j).wait_recv()
+        meta = meta_ref[d * n_ctx + j * INNER + y]
+        total = jnp.zeros((meta.shape[1], width), jnp.float32)
+        for e in range(local):
+            for owner, held in (
+                (c, mine[j * INNER + y, 1, e]), (side, side_land[j, e])
+            ):
+                masks = slot_masks(meta, picks, cap, (owner * local + e) * cap)
+                pick = sum(jnp.where(mask, 1.0, 0.0) for mask in masks)
+                total = total + jnp.dot(
+                    pick.T.astype(jnp.bfloat16), held, preferred_element_type=jnp.float32
+                )
+        return total
+
+    def combine(j):
+        total = spread(j)
+
+        def through(keep):
+            running[j] = keep.astype(jnp.bfloat16)
+            pass_on(j, lambda copy: copy.start())
+
+        arrives = jnp.where(j > z, z > 0, z < length - 1)
+
+        @pl.when(arrives)
         def _():
-            ring(k, True).start()
-
-        return carry
-
-    lax.fori_loop(0, n_ctx, inward, 0)
-    own = pltpu.make_async_copy(done.at[0], out_ref.at[c], own_sem)
-    own.start()
-    lax.fori_loop(n_ctx * units // gaps, units, unit, 0)
-    own.wait()
+            along(j, True, j).wait_recv()
+            through(total + widen(land[j]))
+
+        @pl.when(jnp.logical_not(arrives))
+        def _():
+            through(total)
+
+    def finish(i):
+        out_tok[...] = spread(z)
+        for slot, there in ((z, z > 0), (length, z < length - 1)):
+
+            @pl.when(there)
+            def _(slot=slot):
+                along(z, True, slot).wait_recv()
+                out_tok[...] = out_tok[...] + widen(land[slot])
+
+    def turn(i, carry):
+        r = length - 1 - i
+        each(r, inward)
+        lax.fori_loop(lax.div(i * units, length), lax.div((i + 1) * units, length), unit, 0)
+        each(r, combine)
+        return carry
+
+    lax.fori_loop(0, length - 1, turn, 0)
+    inward(z)
+    lax.fori_loop(lax.div((length - 1) * units, length), units, unit, 0)
+    finish(0)
     lax.fori_loop(1, n, score_finish, 0)
 
-    def drain(k, carry):
-        to_sib(k, 0).wait_send()
-        to_sib(k, 1).wait_send()
-        to_far(k).wait_send()
-
-        @pl.when(k > 0)
-        def _():
-            ring(k, True).wait_send()
-            ring(k, False).wait_recv()
-
-        return carry
-
-    lax.fori_loop(0, n_ctx, drain, 0)
+    def drain(j):
+        for owner in (j * INNER + 1 - y, j * INNER + y):
+            to_sib(owner, 0).wait_send()
+            to_sib(owner, 1).wait_send()
+            to_far(owner).wait_send()
+        to_side(j).wait_send()
+        pass_on(j, lambda copy: copy.wait_send())
+
+    outermost(drain)
 
     def store_wait(u, carry):
         for copy in results(u):
@@ -699,31 +800,36 @@
     lax.fori_loop(0, units, store_wait, 0)
 
 
-def return_rows(back, rows, grad, pair, hidden, score, n_dp, n_ctx):
+def return_rows(back, rows, grad, pair, hidden, score, meta, n_dp, n_ctx):
     local, total, width = back.shape
-    cap = total // (n_dp * n_ctx)
+    n = n_dp * n_ctx
+    cap = total // n
+    length = n_ctx // INNER
+    tokens = meta.shape[2]
     depth = hidden.shape[2]
     tile = 256 if width % 256 == 0 else 128
     units = local * (width // tile)
     block = (local, cap, width)
     low = back.dtype
+    dma = pltpu.SemaphoreType.DMA
     return pl.pallas_call(
         functools.partial(return_kernel, n_dp, n_ctx, cap, tile),
         out_shape=(
-            jax.ShapeDtypeStruct((n_ctx,) + block, low),
             jax.ShapeDtypeStruct((local, width, depth), low),
             jax.ShapeDtypeStruct((local, width, depth), low),
             jax.ShapeDtypeStruct((local, depth, width), low),
             jax.ShapeDtypeStruct(score.shape, jnp.float32),
+            jax.ShapeDtypeStruct((tokens, width), jnp.float32),
         ),
-        in_specs=[ANY] * 5 + [VMEM],
-        out_specs=(ANY,) * 4 + (VMEM,),
+        in_specs=[ANY] * 5 + [VMEM] * 2,
+        out_specs=(ANY,) * 3 + (VMEM,) * 2,
         scratch_shapes=[
             pltpu.VMEM((n_ctx, 2) + block, low),
             pltpu.VMEM((n_ctx, 2) + block, low),
             pltpu.VMEM((n_ctx,) + block, low),
-            pltpu.VMEM((n_ctx,) + block, low),
-            pltpu.VMEM((n_ctx,) + block, low),
+            pltpu.VMEM((length,) + block, low),
+            pltpu.VMEM((length, tokens, width), low),
+            pltpu.VMEM((length + 1, tokens, width), low),
             pltpu.VMEM((local, total, 2 * depth), low),
             pltpu.VMEM((local, total, depth), low),
             pltpu.VMEM((local, depth, total), low),
@@ -731,24 +837,25 @@
             pltpu.VMEM((2, total, tile), low),
             pltpu.VMEM((units, tile, 2 * depth), low),
             pltpu.VMEM((units, depth, tile), low),
-            pltpu.SemaphoreType.DMA((n_ctx, 2)),
-            pltpu.SemaphoreType.DMA((n_ctx, 2)),
-            pltpu.SemaphoreType.DMA((n_ctx, 2)),
-            pltpu.SemaphoreType.DMA((n_ctx,)),
-            pltpu.SemaphoreType.DMA((n_ctx,)),
-            pltpu.SemaphoreType.DMA((n_ctx,)),
-            pltpu.SemaphoreType.DMA((n_ctx,)),
-            pltpu.SemaphoreType.DMA,
-            pltpu.SemaphoreType.DMA((2,)),
-            pltpu.SemaphoreType.DMA((2, 2)),
-            pltpu.SemaphoreType.DMA((3, units)),
-            pltpu.SemaphoreType.DMA((n_dp * n_ctx,)),
-            pltpu.SemaphoreType.DMA((n_dp * n_ctx,)),
+            dma((n_ctx, 2)),
+            dma((n_ctx, 2)),
+            dma((n_ctx, 2)),
+            dma((n_ctx,)),
+            dma((n_ctx,)),
+            dma((length,)),
+            dma((length,)),
+            dma((length,)),
+            dma((length + 1,)),
+            dma((2,)),
+            dma((2, 2)),
+            dma((3, units)),
+            dma((n,)),
+            dma((n,)),
         ],
         compiler_params=pltpu.CompilerParams(
-            collective_id=1, has_side_effects=True, vmem_limit_bytes=60 * 1024 * 1024
+            collective_id=1, has_side_effects=True, vmem_limit_bytes=63 * 1024 * 1024
         ),
-    )(back, rows, grad, pair, hidden, score)
+    )(back, rows, grad, pair, hidden, score, meta)
 
 
 def tiles(x):
@@ -768,7 +875,6 @@
     width = tokens.shape[1]
     capacity = max(2, rows_here * picks * 5 // (4 * experts))
     capacity = -(-capacity // 8) * 8
-    slots = experts * capacity
     widened = tokens.astype(jnp.float32)
     inverse = lax.rsqrt(jnp.mean(widened * widened, axis=1, keepdims=True) + EPSILON)
     scaled = widened * inverse
@@ -785,18 +891,13 @@
     rank = jnp.sum(jnp.where(member, count[:, None, :], 0.0), axis=2)
     position = expert_ids.astype(jnp.float32) * capacity + rank
     meta = jnp.concatenate([position, gates], axis=1).T[None]
-    rows, upstream, pair, hidden, back, score = dispatch_rows(
+    rows, upstream, pair, hidden, back, score, metas = dispatch_rows(
         normed, cotangent, meta, gate_weight, up_weight, down_weight, capacity, n_dp, n_ctx
     )
-    back_slots, gate_grad, up_grad, down_grad, score_parts = return_rows(
-        back, rows, upstream, pair, hidden, score, n_dp, n_ctx
+    gate_grad, up_grad, down_grad, score_parts, grad_tok = return_rows(
+        back, rows, upstream, pair, hidden, score, metas, n_dp, n_ctx
     )
     score_tok = jnp.sum(score_parts, axis=0)[:picks].T
-    back_flat = back_slots.reshape(slots, width)
-    places = jnp.arange(slots, dtype=jnp.float32)[:, None]
-    match = [places == position[:, k][None, :] for k in range(picks)]
-    dispatch_low = sum(jnp.where(hit, 1.0, 0.0) for hit in match).astype(jnp.bfloat16)
-    grad_tok = jnp.dot(dispatch_low.T, back_flat, preferred_element_type=jnp.float32)
     mixed = jnp.sum(gates * score_tok, axis=1, keepdims=True)
     grad_chosen = gates * (score_tok - mixed)
     grad_logits = jnp.sum(jnp.where(member, grad_chosen[:, :, None], 0.0), axis=1).astype(

time: 245 us -> 223 us (0.910)
  Pallas kernels: 222 us -> 199 us
    pallas_call x1, Pallas kernels: 136 us -> 114 us  [dispatch_rows(): pl.pallas_call(functools.partial(dispatch_kernel, n_dp, n_ctx, cap), out_...]
    pallas_call x1, Pallas kernels: 68.7 us -> 74.6 us  [return_rows(): pl.pallas_call(functools.partial(return_kernel, n_dp, n_ctx, cap, tile),...]
    pallas_call x1, Pallas kernels: 16.4 us -> 10.9 us  [exchange(): pl.pallas_call(functools.partial(exchange_kernel, n_dp, n_ctx, keep), out...]
    unnamed x25 -> x23, local copies, waits for them, and re-layouts: 9.45 us -> 9.45 us
where the time goes in v2:
time: 223 us; the launch traced here: 222 us
  Pallas kernels  199 us (89%)
  local copies, waits for them, and re-layouts  11.8 us (5%)
  other arithmetic  7.43 us (3%)
  matrix products  2.4 us (1%)
    pallas_call x1, Pallas kernels, dispatch_rows(): pl.pallas_call(functools.partial(dispatch_kernel, n_dp, n_ctx, cap), out_...  114 us
    pallas_call x1, Pallas kernels, return_rows(): pl.pallas_call(functools.partial(return_kernel, n_dp, n_ctx, cap, tile),...  74.6 us
    pallas_call x1, Pallas kernels, exchange(): pl.pallas_call(functools.partial(exchange_kernel, n_dp, n_ctx, keep), out...  10.9 us
    unnamed x23, local copies, waits for them, and re-layouts  9.45 us

profile of v2, /device:TPU:0, one launch (start us, length us, event | category | flops | bytes accessed | tf_op | source)
XLA Modules:
  0.0 221.8 jit_solution(16941390148179379503)
XLA Ops:
  0.6 1.2 fusion.11
  1.9 0.7 fusion.17
  2.6 0.2 fusion.14
  2.8 1.2 fusion.4.rows_ref
  4.0 0.2 fusion.27
  4.2 0.8 select_reduce_fusion.2
  5.0 0.7 multiply_add_fusion
  5.7 0.6 maximum_bitcast_fusion.meta_ref
  6.3 113.8 %shard_map.127 = (bf16[2,1280,1792]{2,1,0:T(8,128)(2,1)}, bf16[2,1280,1792]{2,1,0:T(8,128)(2,1)}, bf16[2,1280,768]{2,1,0:T(8,128)(2,1)}, bf16[2,1280,384]{2,1,0:...) custom-call(bf16[128,1792]{1,0:T(8,128)(2,1)} %copy-done.2, ...), custom_call_target="tpu_custom_call" | custom-call | tf_op jit(solution)/shard_map/pallas_call | solution.py:492
  120.2 74.6 %shard_map.128 = (bf16[2,1792,384]{2,1,0:T(8,128)(2,1)}, bf16[2,1792,384]{2,1,0:T(8,128)(2,1)}, bf16[2,384,1792]{2,1,0:T(8,128)(2,1)}, f32[32,8,128]{2,1,0:T(8,128)}, f32[128,1792]{1,0:T(8,128)}) custom-call(bf16[2,1280,1792]{2,1,0:T(8,128)(2,1)} %get-tuple-element.18.back_ref, bf16[2,1280,1792]{2,1,0:T(8,128)(2,1)} %get-tuple-element.19.rows_ref, ...), custom_call_target="tpu_custom_call" | custom-call | tf_op jit(solution)/shard_map/pallas_call | solution.py:815
  194.8 1.0 reduce_sum.85
  195.9 1.7 fusion.10
  197.6 1.1 fusion.9
  198.9 0.3 fusion.28
  199.2 0.3 reshape.48
  199.5 0.7 copy.28
  200.2 10.9 %shard_map.129 = f32[1,8,128]{2,1,0:T(8,128)} custom-call(f32[32,8,128]{2,1,0:T(8,128)} %bitcast.23), custom_call_target="tpu_custom_call" | custom-call | tf_op jit(solution)/shard_map/pallas_call | solution.py:76
  211.1 1.2 slice.12
  212.3 0.8 reshape.51
  213.0 0.7 copy.26
  213.7 3.7 %copy.32 = bf16[2,1792,384]{2,1,0:T(8,128)(2,1)} copy(bf16[2,1792,384]{2,1,0:T(8,128)(2,1)} %get-tuple-element.62) | data formatting | bytes 5505024
  217.5 1.5 copy.33
  219.0 1.2 copy-done.4
  220.2 1.5 copy.34
  (26 shorter events, 0.2 us)
Async XLA Ops:
  0.6 3.4 %copy-start = (bf16[1792,16]{0,1:T(8,128)(2,1)S(1)}, bf16[1792,16]{0,1:T(8,128)(2,1)}, u32[]{:S(2)}) copy-start(bf16[1792,16]{0,1:T(8,128)(2,1)} %param.12) | copy-start | bytes 172036
  4.0 2.3 %copy-start.2 = (bf16[128,1792]{1,0:T(8,128)(2,1)}, bf16[128,1792]{1,0:T(8,128)(2,1)S(1)}, u32[]{:S(2)}) copy-start(bf16[128,1792]{1,0:T(8,128)(2,1)S(1)} %fusion.4.rows_ref) | copy-start | bytes 1376260
  120.1 75.8 %copy-start.8 = (s32[128,4]{0,1:T(4,128)S(1)}, s32[128,4]{0,1:T(4,128)}, u32[]{:S(2)}) copy-start(s32[128,4]{0,1:T(4,128)} %param.10) | copy-start | bytes 6148
  120.1 75.8 %copy-start.1 = (bf16[128,1792]{1,0:T(8,128)(2,1)S(1)}, bf16[128,1792]{1,0:T(8,128)(2,1)}, u32[]{:S(2)}) copy-start(bf16[128,1792]{1,0:T(8,128)(2,1)} %param.8) | copy-start | bytes 1376260
  120.1 75.8 %copy-start.7 = (f32[1792]{0:T(1024)S(1)}, f32[1792]{0:T(1024)}, u32[]{:S(2)}) copy-start(f32[1792]{0:T(1024)} %param.11) | copy-start | bytes 21508
  194.8 2.8 %copy-start.6 = (bf16[128,1792]{1,0:T(8,128)(2,1)S(1)}, bf16[128,1792]{1,0:T(8,128)(2,1)}, u32[]{:S(2)}) copy-start(bf16[128,1792]{1,0:T(8,128)(2,1)} %grad_ref.1) | copy-start | bytes 1376260
  194.8 4.0 %copy-start.3 = (bf16[128,1792]{1,0:T(8,128)(2,1)S(1)}, bf16[128,1792]{1,0:T(8,128)(2,1)}, u32[]{:S(2)}) copy-start(bf16[128,1792]{1,0:T(8,128)(2,1)} %copy-done.2) | copy-start | bytes 1376260
  213.7 3.7 %copy-start.5 = (bf16[2,1792,384]{2,1,0:T(8,128)(2,1)S(1)}, bf16[2,1792,384]{2,1,0:T(8,128)(2,1)}, u32[]{:S(2)}) copy-start(bf16[2,1792,384]{2,1,0:T(8,128)(2,1)} %get-tuple-element.63) | copy-start | bytes 8257540
  217.5 2.8 %copy-start.4 = (bf16[2,384,1792]{2,1,0:T(8,128)(2,1)S(1)}, bf16[2,384,1792]{2,1,0:T(8,128)(2,1)}, u32[]{:S(2)}) copy-start(bf16[2,384,1792]{2,1,0:T(8,128)(2,1)} %get-tuple-element.64) | copy-start | bytes 8257540

commit v3 on v2

--- a/solution.py
+++ b/solution.py
@@ -718,14 +718,16 @@
         hid[e] = hid_raw[e].T
 
     def inward(j):
-        for owner in (j * INNER + 1 - y, j * INNER + y):
+        theirs = j * INNER + 1 - y
+        for owner in (theirs, j * INNER + y):
             to_sib(owner, 1).wait_recv()
             load(owner, 1).wait()
             to_far(owner).wait_recv()
             mine[owner, 1] = (
                 widen(mine[owner, 1]) + widen(sib_land[owner, 1]) + widen(far_land[owner])
             ).astype(jnp.bfloat16)
-        to_side(j).start()
+            if owner is theirs:
+                to_side(j).start()
 
     def spread(j):
         to_side(j).wait_recv()
@@ -858,6 +860,76 @@
     )(back, rows, grad, pair, hidden, score, meta)
 
 
+def finish_kernel(
+    tok_ref, cot_ref, norm_ref, gain_ref, router_ref, ids_ref, meta_ref, score_ref, grad_ref,
+    gate_ref, up_ref, down_ref, out_tok, sums, gate_out, up_out, down_out,
+    gate_held, up_held, down_held, load_sem, store_sem,
+):
+    local, picks = gate_ref.shape[0], ids_ref.shape[0]
+    experts = router_ref.shape[0]
+    moved = ((gate_ref, gate_held, gate_out), (up_ref, up_held, up_out))
+    moved = moved + ((down_ref, down_held, down_out),)
+    loads = [
+        pltpu.make_async_copy(src.at[e], held.at[e], load_sem.at[i, e])
+        for i, (src, held, _) in enumerate(moved)
+        for e in range(local)
+    ]
+    stores = [
+        pltpu.make_async_copy(held.at[e], out.at[e], store_sem.at[i, e])
+        for i, (_, held, out) in enumerate(moved)
+        for e in range(local)
+    ]
+    for load in loads:
+        load.start()
+    score = jnp.sum(score_ref[...], axis=0)[:picks]
+    gates = meta_ref[picks : 2 * picks]
+    mixed = jnp.sum(gates * score, axis=0, keepdims=True)
+    grad_chosen = gates * (score - mixed)
+    labels = lax.broadcasted_iota(jnp.int32, (experts, score.shape[1]), 0)
+    grad_logits = sum(
+        jnp.where(ids_ref[k : k + 1] == labels, grad_chosen[k : k + 1], 0.0) for k in range(picks)
+    )
+    sums[:experts] = jnp.dot(
+        grad_logits.astype(jnp.bfloat16), norm_ref[...], preferred_element_type=jnp.float32
+    )
+    for load, store in zip(loads, stores):
+        load.wait()
+        store.start()
+    grad_normed = grad_ref[...] + jnp.dot(
+        grad_logits.T.astype(jnp.bfloat16), router_ref[...], preferred_element_type=jnp.float32
+    )
+    widened = tok_ref[...].astype(jnp.float32)
+    inverse = lax.rsqrt(jnp.mean(widened * widened, axis=1, keepdims=True) + EPSILON)
+    scaled = widened * inverse
+    gained = jnp.sum(grad_normed * scaled, axis=0, keepdims=True)
+    sums[experts:] = jnp.broadcast_to(gained, (8, gained.shape[1]))
+    grad_scaled = grad_normed * gain_ref[...]
+    correction = jnp.mean(grad_scaled * scaled, axis=1, keepdims=True)
+    out_tok[...] = (
+        cot_ref[...].astype(jnp.float32) + inverse * (grad_scaled - scaled * correction)
+    ).astype(jnp.bfloat16)
+    for store in stores:
+        store.wait()
+
+
+def finish_rows(values, weights):
+    tokens, router = values[0], values[4]
+    dma = pltpu.SemaphoreType.DMA
+    return pl.pallas_call(
+        finish_kernel,
+        out_shape=(
+            jax.ShapeDtypeStruct(tokens.shape, tokens.dtype),
+            jax.ShapeDtypeStruct((router.shape[0] + 8, router.shape[1]), jnp.float32),
+        )
+        + tuple(jax.ShapeDtypeStruct(weight.shape, weight.dtype) for weight in weights),
+        in_specs=[VMEM] * len(values) + [ANY] * 3,
+        out_specs=(VMEM, VMEM) + (ANY,) * 3,
+        scratch_shapes=[pltpu.VMEM(weight.shape, weight.dtype) for weight in weights]
+        + [dma((3, weights[0].shape[0]))] * 2,
+        compiler_params=pltpu.CompilerParams(vmem_limit_bytes=60 * 1024 * 1024),
+    )(*values, *weights)
+
+
 def tiles(x):
     return jnp.pad(x, ((0, 0), (0, 1024 - x.shape[1]))).reshape(x.shape[0], 8, 128)
 
@@ -897,17 +969,11 @@
     gate_grad, up_grad, down_grad, score_parts, grad_tok = return_rows(
         back, rows, upstream, pair, hidden, score, metas, n_dp, n_ctx
     )
-    score_tok = jnp.sum(score_parts, axis=0)[:picks].T
-    mixed = jnp.sum(gates * score_tok, axis=1, keepdims=True)
-    grad_chosen = gates * (score_tok - mixed)
-    grad_logits = jnp.sum(jnp.where(member, grad_chosen[:, :, None], 0.0), axis=1).astype(
-        jnp.bfloat16
-    )
-    grad_normed = grad_tok + jnp.dot(
-        grad_logits, router_weight.T, preferred_element_type=jnp.float32
-    )
-    router_part = jnp.dot(normed.T, grad_logits, preferred_element_type=jnp.float32)
-    gain_part = jnp.sum(grad_normed * scaled, axis=0)
+    values = (tokens, cotangent, normed, norm_gain[None], router_weight.T, expert_ids.T)
+    grad_input, total, gate_grad, up_grad, down_grad = finish_rows(
+        values + (meta[0], score_parts, grad_tok), (gate_grad, up_grad, down_grad)
+    )
+    router_part, gain_part = total[:experts].T, total[experts]
     share = width // n
     parts = jnp.concatenate(
         [router_part.reshape(n, share * experts), gain_part.reshape(n, share)], axis=1
@@ -915,11 +981,6 @@
     sums = exchange(tiles(parts), n_dp, n_ctx, 1, 3).reshape(1024)
     router_grad = sums[: share * experts].reshape(share, experts)
     gain_grad = sums[share * experts : share * experts + share]
-    grad_scaled = grad_normed * norm_gain
-    correction = jnp.mean(grad_scaled * scaled, axis=1, keepdims=True)
-    grad_input = (
-        cotangent.astype(jnp.float32) + inverse * (grad_scaled - scaled * correction)
-    ).astype(jnp.bfloat16)
     return (grad_input, gate_grad, up_grad, down_grad, router_grad, gain_grad)
 
 

time: 223 us -> 220 us (0.987)
  Pallas kernels: 199 us -> 206 us
  local copies, waits for them, and re-layouts: 11.8 us -> 6.28 us
    pallas_call x0 -> x1, Pallas kernels: none -> 9.08 us  [finish_rows(): pl.pallas_call(finish_kernel, out_shape=(jax.ShapeDtypeStruct(tokens.shap...]
    unnamed x23 -> x6, local copies, waits for them, and re-layouts: 9.45 us -> 1.35 us
where the time goes in v3:
time: 220 us; the launch traced here: 219 us
  Pallas kernels  206 us (94%)
  local copies, waits for them, and re-layouts  6.28 us (3%)
  other arithmetic  5.22 us (2%)
    pallas_call x1, Pallas kernels, dispatch_rows(): pl.pallas_call(functools.partial(dispatch_kernel, n_dp, n_ctx, cap), out_...  113 us
    pallas_call x1, Pallas kernels, return_rows(): pl.pallas_call(functools.partial(return_kernel, n_dp, n_ctx, cap, tile),...  72.6 us
    pallas_call x1, Pallas kernels, exchange(): pl.pallas_call(functools.partial(exchange_kernel, n_dp, n_ctx, keep), out...  10.6 us
    pallas_call x1, Pallas kernels, finish_rows(): pl.pallas_call(finish_kernel, out_shape=(jax.ShapeDtypeStruct(tokens.shap...  9.08 us

profile of v3, /device:TPU:0, one launch (start us, length us, event | category | flops | bytes accessed | tf_op | source)
XLA Modules:
  0.0 219.3 jit_solution(7530576632854746738)
XLA Ops:
  0.6 1.2 fusion
  1.8 1.2 fusion.2.rows_ref.norm_ref
  3.0 0.0 copy-start
  3.0 1.1 fusion.15
  4.1 0.8 fusion.8
  4.9 0.2 fusion.5
  5.1 0.7 select_reduce_fusion.1
  5.8 0.7 multiply_add_fusion
  6.5 0.6 fusion.11
  7.1 113.5 %shard_map.127 = (bf16[2,1280,1792]{2,1,0:T(8,128)(2,1)}, bf16[2,1280,1792]{2,1,0:T(8,128)(2,1)}, bf16[2,1280,768]{2,1,0:T(8,128)(2,1)}, bf16[2,1280,384]{2,1,0:...) custom-call(bf16[128,1792]{1,0:T(8,128)(2,1)} %copy-done, ...), custom_call_target="tpu_custom_call" | custom-call | tf_op jit(solution)/shard_map/pallas_call | solution.py:492
  120.6 0.0 copy-start.1
  120.6 72.6 %shard_map.128 = (bf16[2,1792,384]{2,1,0:T(8,128)(2,1)}, bf16[2,1792,384]{2,1,0:T(8,128)(2,1)}, bf16[2,384,1792]{2,1,0:T(8,128)(2,1)}, f32[32,8,128]{2,1,0:T(8,128)}, f32[128,1792]{1,0:T(8,128)}) custom-call(bf16[2,1280,1792]{2,1,0:T(8,128)(2,1)} %get-tuple-element.23.back_ref, bf16[2,1280,1792]{2,1,0:T(8,128)(2,1)} %get-tuple-element.24.rows_ref, ...), custom_call_target="tpu_custom_call" | custom-call | tf_op jit(solution)/shard_map/pallas_call | solution.py:817
  193.2 0.6 broadcast_in_dim.38.gain_ref
  193.8 9.1 %shard_map.129 = (bf16[128,1792]{1,0:T(8,128)(2,1)}, f32[24,1792]{1,0:T(8,128)}, bf16[2,1792,384]{2,1,0:T(8,128)(2,1)}, bf16[2,1792,384]{2,1,0:T(8,128)(2,1)}, bf16[2,384,1792]{2,1,0:T(8,128)(2,1)}) custom-call(bf16[128,1792]{1,0:T(8,128)(2,1)} %tok_ref.1, bf16[128,1792]{1,0:T(8,128)(2,1)} %cot_ref.1, bf16[128,1792]{1,0:T(8,128)(2,1)} %copy-done, ...), custom_call_target="tpu_custom_call" | custom-call | tf_op jit(solution)/shard_map/pallas_call | solution.py:918
  202.9 0.9 slice_bitcast_fusion
  203.8 0.3 copy.23
  204.1 0.3 reshape.39
  204.4 0.8 slice_reduce_fusion
  205.3 0.1 reshape_squeeze.3
  205.4 0.7 copy.25
  206.0 10.6 %shard_map.130 = f32[1,8,128]{2,1,0:T(8,128)} custom-call(f32[32,8,128]{2,1,0:T(8,128)} %bitcast.17), custom_call_target="tpu_custom_call" | custom-call | tf_op jit(solution)/shard_map/pallas_call | solution.py:76
  216.7 0.7 reshape.41
  217.4 0.7 copy.24
  218.1 1.2 slice.16
  (6 shorter events, 0.1 us)
Async XLA Ops:
  3.0 4.1 %copy-start = (bf16[128,1792]{1,0:T(8,128)(2,1)}, bf16[128,1792]{1,0:T(8,128)(2,1)S(1)}, u32[]{:S(2)}) copy-start(bf16[128,1792]{1,0:T(8,128)(2,1)S(1)} %fusion.2.rows_ref.norm_ref) | copy-start | bytes 1376260
  120.6 72.6 %copy-start.1 = (f32[1792]{0:T(1024)S(1)}, f32[1792]{0:T(1024)}, u32[]{:S(2)}) copy-start(f32[1792]{0:T(1024)} %param.11) | copy-start | bytes 21508

commit v4 on v3

--- a/solution.py
+++ b/solution.py
@@ -429,13 +429,13 @@
         first_half(ready)
         each(r, lambda j: arrive(1, j))
         each(r, lambda j: take_side(0, j))
-        second_half(ready)
 
         @pl.when(core == 0)
         def _():
             each(r, lambda j: arrive(2, j))
             each(r, lambda j: take_side(1, j))
 
+        second_half(ready)
         return carry
 
     take_side(0, z)

time: 220 us -> 218 us (level)
  Pallas kernels: 206 us -> 203 us
    pallas_call x1, Pallas kernels: 72.6 us -> 66.5 us  [return_rows(): pl.pallas_call(functools.partial(return_kernel, n_dp, n_ctx, cap, tile),...]
    pallas_call x1, Pallas kernels: 113 us -> 117 us  [dispatch_rows(): pl.pallas_call(functools.partial(dispatch_kernel, n_dp, n_ctx, cap), out_...]
where the time goes in v4:
time: 218 us; the launch traced here: 217 us
  Pallas kernels  203 us (93%)
  local copies, waits for them, and re-layouts  6.28 us (3%)
  other arithmetic  5.22 us (2%)
    pallas_call x1, Pallas kernels, dispatch_rows(): pl.pallas_call(functools.partial(dispatch_kernel, n_dp, n_ctx, cap), out_...  117 us
    pallas_call x1, Pallas kernels, return_rows(): pl.pallas_call(functools.partial(return_kernel, n_dp, n_ctx, cap, tile),...  66.5 us
    pallas_call x1, Pallas kernels, exchange(): pl.pallas_call(functools.partial(exchange_kernel, n_dp, n_ctx, keep), out...  10.6 us
    pallas_call x1, Pallas kernels, finish_rows(): pl.pallas_call(finish_kernel, out_shape=(jax.ShapeDtypeStruct(tokens.shap...  9.08 us

profile of v4, /device:TPU:0, one launch (start us, length us, event | category | flops | bytes accessed | tf_op | source)
XLA Modules:
  0.0 216.6 jit_solution(5737540980090558705)
XLA Ops:
  0.6 1.2 fusion
  1.8 1.2 fusion.2.rows_ref.norm_ref
  3.0 0.0 copy-start
  3.0 1.1 fusion.15
  4.1 0.8 fusion.8
  4.9 0.2 fusion.5
  5.1 0.7 select_reduce_fusion.1
  5.8 0.7 multiply_add_fusion
  6.5 0.6 fusion.11
  7.1 117.0 %shard_map.127 = (bf16[2,1280,1792]{2,1,0:T(8,128)(2,1)}, bf16[2,1280,1792]{2,1,0:T(8,128)(2,1)}, bf16[2,1280,768]{2,1,0:T(8,128)(2,1)}, bf16[2,1280,384]{2,1,0:...) custom-call(bf16[128,1792]{1,0:T(8,128)(2,1)} %copy-done, ...), custom_call_target="tpu_custom_call" | custom-call | tf_op jit(solution)/shard_map/pallas_call | solution.py:492
  124.1 0.0 copy-start.1
  124.1 66.5 %shard_map.128 = (bf16[2,1792,384]{2,1,0:T(8,128)(2,1)}, bf16[2,1792,384]{2,1,0:T(8,128)(2,1)}, bf16[2,384,1792]{2,1,0:T(8,128)(2,1)}, f32[32,8,128]{2,1,0:T(8,128)}, f32[128,1792]{1,0:T(8,128)}) custom-call(bf16[2,1280,1792]{2,1,0:T(8,128)(2,1)} %get-tuple-element.23.back_ref, bf16[2,1280,1792]{2,1,0:T(8,128)(2,1)} %get-tuple-element.24.rows_ref, ...), custom_call_target="tpu_custom_call" | custom-call | tf_op jit(solution)/shard_map/pallas_call | solution.py:817
  190.6 0.6 broadcast_in_dim.38.gain_ref
  191.2 9.1 %shard_map.129 = (bf16[128,1792]{1,0:T(8,128)(2,1)}, f32[24,1792]{1,0:T(8,128)}, bf16[2,1792,384]{2,1,0:T(8,128)(2,1)}, bf16[2,1792,384]{2,1,0:T(8,128)(2,1)}, bf16[2,384,1792]{2,1,0:T(8,128)(2,1)}) custom-call(bf16[128,1792]{1,0:T(8,128)(2,1)} %tok_ref.1, bf16[128,1792]{1,0:T(8,128)(2,1)} %cot_ref.1, bf16[128,1792]{1,0:T(8,128)(2,1)} %copy-done, ...), custom_call_target="tpu_custom_call" | custom-call | tf_op jit(solution)/shard_map/pallas_call | solution.py:918
  200.3 0.9 slice_bitcast_fusion
  201.2 0.3 copy.23
  201.5 0.3 reshape.39
  201.8 0.8 slice_reduce_fusion
  202.6 0.1 reshape_squeeze.3
  202.7 0.7 copy.25
  203.4 10.6 %shard_map.130 = f32[1,8,128]{2,1,0:T(8,128)} custom-call(f32[32,8,128]{2,1,0:T(8,128)} %bitcast.17), custom_call_target="tpu_custom_call" | custom-call | tf_op jit(solution)/shard_map/pallas_call | solution.py:76
  214.0 0.7 reshape.41
  214.7 0.7 copy.24
  215.4 1.2 slice.16
  (6 shorter events, 0.1 us)
Async XLA Ops:
  3.0 4.1 %copy-start = (bf16[128,1792]{1,0:T(8,128)(2,1)}, bf16[128,1792]{1,0:T(8,128)(2,1)S(1)}, u32[]{:S(2)}) copy-start(bf16[128,1792]{1,0:T(8,128)(2,1)S(1)} %fusion.2.rows_ref.norm_ref) | copy-start | bytes 1376260
  124.1 66.5 %copy-start.1 = (f32[1792]{0:T(1024)S(1)}, f32[1792]{0:T(1024)}, u32[]{:S(2)}) copy-start(f32[1792]{0:T(1024)} %param.11) | copy-start | bytes 21508
